TPU v7x, 8 devices: a whole 2x2x1 slice. The times are simulated.
8 devices in a mesh: data: 2 (over z, y), stage: 4 (over x, core).
Axes of the slice: x: 2, y: 2, z: 1, core: 2. Of those that a mesh axis runs over, the one named last changes fastest.
Arguments:
- master_up: float32 [4, 768, 3072], P('stage')
- master_down: float32 [4, 3072, 768], P('stage')
- mom1_up: float32 [4, 768, 3072], P('stage')
- mom1_down: float32 [4, 3072, 768], P('stage')
- mom2_up: float32 [4, 768, 3072], P('stage')
- mom2_down: float32 [4, 3072, 768], P('stage')
- grad_up: float32 [2, 4, 768, 3072], P('data', 'stage')
- grad_down: float32 [2, 4, 3072, 768], P('data', 'stage')
- stage_acts: bfloat16 [4, 8192, 768], P('stage', 'data')
- loss_grad: bfloat16 [8192, 768], P('data')
- next_batch: bfloat16 [2, 8192, 768], P(None, 'data')
- learn_rate: float32 [], replicated
- max_norm: float32 [], replicated
Outputs:
- output 1: float32 [4, 768, 3072], P('stage')
- output 2: float32 [4, 3072, 768], P('stage')
- output 3: float32 [4, 768, 3072], P('stage')
- output 4: float32 [4, 3072, 768], P('stage')
- output 5: float32 [4, 768, 3072], P('stage')
- output 6: float32 [4, 3072, 768], P('stage')
- output 7: bfloat16 [4, 2, 8192, 768], P('stage', None, 'data')
All inputs are finite; a program needn't handle non-finite values.
Results may differ from a plain program's by a relative error of at most 0.00896169.
Values are sent between devices in bfloat16 or wider.
A program may use at most 1 GiB of HBM per device.

v0:
```python
import functools

import jax
import jax.numpy as jnp
from jax import lax
from jax.experimental import pallas as pl
from jax.experimental.pallas import tpu as pltpu
from jax.sharding import PartitionSpec as P


BETA1 = 0.9
BETA2 = 0.95
ADAM_EPS = 1e-8
WEIGHT_DECAY = 0.1
NORM_EPS = 1e-6
ADAM_STEP = 8
SQRT_TWO_PI = 0.7978845608028654
GELU_CUBIC = 0.044715

BACK_ROWS = 256
FWD_ROWS = 256
BACK_TILE = 512
FWD_TILE = 512
PIECES = 6
F32_FIRST = ((0, 0),)
TAIL = ((0, 1, 5), (1, 0, 5), (0, 5, 6), (1, 5, 6))
STAGING = 4
WGRAD_STEP = 1024
WGRAD_GRID = 2
UPDATE_GRID = 4

BF16 = jnp.bfloat16
F32 = jnp.float32
MESH_ID = pl.DeviceIdType.MESH
ANY = pl.BlockSpec(memory_space=pl.ANY)
VMEM_LIMIT = 60 * 1024 * 1024
FWD_VMEM = 54000000
STORE_VMEM = 4 * 1024 * 1024
UPDATE_VMEM = 60 * 1024 * 1024


def dot_nn(left, right):
    return lax.dot_general(left, right, (((1,), (0,)), ((), ())), preferred_element_type=F32)


def dot_nt(left, right):
    return lax.dot_general(left, right, (((1,), (1,)), ((), ())), preferred_element_type=F32)


def dot_tn(left, right):
    return lax.dot_general(left, right, (((0,), (0,)), ((), ())), preferred_element_type=F32)


def span(index, size):
    return pl.ds(pl.multiple_of(index * size, size), size)


def tanh_part(x, sq):
    return jnp.tanh(x * (SQRT_TWO_PI + (SQRT_TWO_PI * GELU_CUBIC) * sq))


def gelu_value(x):
    return x * (0.5 + 0.5 * tanh_part(x, x * x))


def gelu_pair(x):
    sq = x * x
    th = tanh_part(x, sq)
    half = 0.5 + 0.5 * th
    value = x * half
    slope = half + value * (1.0 - th) * (SQRT_TWO_PI + (3.0 * SQRT_TWO_PI * GELU_CUBIC) * sq)
    return value, slope


def meet_neighbours(stage, n_stages):
    barrier = pltpu.get_barrier_semaphore()

    @pl.when(stage > 0)
    def _():
        pl.semaphore_signal(barrier, inc=1, device_id={"stage": stage - 1}, device_id_type=MESH_ID)

    @pl.when(stage < n_stages - 1)
    def _():
        pl.semaphore_signal(barrier, inc=1, device_id={"stage": stage + 1}, device_id_type=MESH_ID)

    pl.semaphore_wait(barrier, jnp.minimum(stage, 1) + jnp.minimum(n_stages - 1 - stage, 1))


def back_kernel(n_stages, acts_ref, dy_ref, up32_ref, down32_ref, hid_ref, dpre_ref, gown_ref,
                up_ref, down_ref, g_buf, h_buf, p_buf, dx_buf, acc_ref, pre_buf, dh_buf, stage_u, stage_v,
                u_sem, v_sem, recv_sem, send_sem, gown_sem, h_sem, p_sem):
    stage = lax.axis_index("stage")
    last = n_stages - 1
    rows_all, width = g_buf.shape
    hidden = up_ref.shape[1]
    n_chunks = rows_all // BACK_ROWS
    n_tiles = hidden // BACK_TILE
    u_rows = stage_u.shape[1]
    v_rows = stage_v.shape[1]
    n_cast = width // u_rows

    def u_copy(i, slot):
        return pltpu.make_async_copy(up32_ref.at[0, span(i, u_rows), :], stage_u.at[slot], u_sem.at[slot])

    def v_copy(i, slot):
        return pltpu.make_async_copy(down32_ref.at[0, span(i, v_rows), :], stage_v.at[slot], v_sem.at[slot])

    for i in range(STAGING):
        u_copy(i, i).start()
        v_copy(i, i).start()

    def rows_of(c):
        return span(c, BACK_ROWS)

    @pl.when(stage == last)
    def _():
        def load(c, carry):
            pltpu.make_async_copy(dy_ref.at[rows_of(c), :], g_buf.at[rows_of(c), :], recv_sem.at[c]).start()
            return carry

        lax.fori_loop(0, n_chunks, load, 0)

    meet_neighbours(stage, n_stages)

    def cast(i, carry):
        slot = lax.rem(i, STAGING)
        u_copy(i, slot).wait()
        up_ref[span(i, u_rows), :] = stage_u[slot].astype(BF16)
        v_copy(i, slot).wait()
        down_ref[span(i, v_rows), :] = stage_v[slot].astype(BF16)

        @pl.when(i + STAGING < n_cast)
        def _():
            u_copy(i + STAGING, slot).start()
            v_copy(i + STAGING, slot).start()

        return carry

    lax.fori_loop(0, n_cast, cast, 0)

    def send_of(c):
        return pltpu.make_async_remote_copy(
            src_ref=dx_buf.at[rows_of(c), :], dst_ref=g_buf.at[rows_of(c), :],
            send_sem=send_sem.at[c], recv_sem=recv_sem.at[c],
            device_id={"stage": stage - 1}, device_id_type=MESH_ID)

    def out_copies(c, slot):
        return (pltpu.make_async_copy(h_buf.at[slot], hid_ref.at[rows_of(c), :], h_sem.at[slot]),
                pltpu.make_async_copy(p_buf.at[slot], dpre_ref.at[rows_of(c), :], p_sem.at[slot]))

    def gown_copy(c):
        return pltpu.make_async_copy(g_buf.at[rows_of(c), :], gown_ref.at[rows_of(c), :], gown_sem.at[c])

    def chunk(c, carry):
        slot = lax.rem(c, 2)
        rows = rows_of(c)

        @pl.when(c >= 2)
        def _():
            for copy in out_copies(c - 2, slot):
                copy.wait()

        pltpu.make_async_copy(dy_ref.at[rows, :], g_buf.at[rows, :], recv_sem.at[c]).wait()
        gown_copy(c).start()

        def products(j):
            cols = pl.ds(j * BACK_TILE, BACK_TILE)
            pre_buf[j % 2] = dot_nn(acts_ref[0, rows, :], up_ref[:, cols])
            dh_buf[j % 2] = dot_nt(g_buf[rows, :], down_ref[cols, :])

        def rest(j):
            cols = pl.ds(j * BACK_TILE, BACK_TILE)
            value, slope = gelu_pair(pre_buf[j % 2])
            h_buf[slot, :, cols] = value.astype(BF16)
            d_pre = (dh_buf[j % 2] * slope).astype(BF16)
            p_buf[slot, :, cols] = d_pre
            part = dot_nt(d_pre, up_ref[:, cols])
            if j == 0:
                acc_ref[...] = g_buf[rows, :].astype(F32) + part
            elif j < n_tiles - 1:
                acc_ref[...] += part
            else:
                dx_buf[rows, :] = (acc_ref[...] + part).astype(BF16)

        products(0)
        for j in range(n_tiles):
            if j + 1 < n_tiles:
                products(j + 1)
            rest(j)
        for copy in out_copies(c, slot):
            copy.start()

        @pl.when(stage > 0)
        def _():
            send_of(c).start()

        return carry

    lax.fori_loop(0, n_chunks, chunk, 0)

    for c in (n_chunks - 2, n_chunks - 1):
        for copy in out_copies(c, c % 2):
            copy.wait()

    def finish(c, carry):
        gown_copy(c).wait()

        @pl.when(stage > 0)
        def _():
            send_of(c).wait_send()

        return carry

    lax.fori_loop(0, n_chunks, finish, 0)


def backward(n_stages, acts, loss_grad, up32, down32):
    _, rows, width = acts.shape
    hidden = up32.shape[2]
    n_chunks = rows // BACK_ROWS
    u_rows, v_rows = width // 12, hidden // 12
    wide = jax.ShapeDtypeStruct((rows, hidden), BF16)
    return pl.pallas_call(
        functools.partial(back_kernel, n_stages),
        name="backward",
        out_shape=(wide, wide, jax.ShapeDtypeStruct((rows, width), BF16)),
        in_specs=[pl.BlockSpec(memory_space=pltpu.VMEM), ANY, ANY, ANY],
        out_specs=(ANY, ANY, ANY),
        scratch_shapes=[
            pltpu.VMEM((width, hidden), BF16),
            pltpu.VMEM((hidden, width), BF16),
            pltpu.VMEM((rows, width), BF16),
            pltpu.VMEM((2, BACK_ROWS, hidden), BF16),
            pltpu.VMEM((2, BACK_ROWS, hidden), BF16),
            pltpu.VMEM((rows, width), BF16),
            pltpu.VMEM((BACK_ROWS, width), F32),
            pltpu.VMEM((2, BACK_ROWS, BACK_TILE), F32),
            pltpu.VMEM((2, BACK_ROWS, BACK_TILE), F32),
            pltpu.VMEM((STAGING, u_rows, hidden), F32),
            pltpu.VMEM((STAGING, v_rows, width), F32),
            pltpu.SemaphoreType.DMA((STAGING,)),
            pltpu.SemaphoreType.DMA((STAGING,)),
            pltpu.SemaphoreType.DMA((n_chunks,)),
            pltpu.SemaphoreType.DMA((n_chunks,)),
            pltpu.SemaphoreType.DMA((n_chunks,)),
            pltpu.SemaphoreType.DMA((2,)),
            pltpu.SemaphoreType.DMA((2,)),
        ],
        compiler_params=pltpu.CompilerParams(collective_id=0, has_side_effects=True, vmem_limit_bytes=VMEM_LIMIT),
        cost_estimate=pl.CostEstimate(flops=6 * rows * width * hidden, bytes_accessed=6 * rows * hidden, transcendentals=rows * hidden),
    )(acts, loss_grad, up32, down32)


def wgrad_kernel(owner_ref, left_ref, right_ref, grad_ref, sum_ref):
    lead = (0,) * (len(left_ref.shape) - 2)
    sum_ref[...] = grad_ref[0, 0]

    def step(k, carry):
        part = span(k, WGRAD_STEP)
        sum_ref[...] += dot_tn(left_ref[lead + (part, slice(None))], right_ref[part, :])
        return carry

    lax.fori_loop(0, right_ref.shape[0] // WGRAD_STEP, step, 0)


def wgrad_call(owner, operands, in_specs, out_spec, shape, steps):
    rows = operands[1].shape[0]
    return pl.pallas_call(
        wgrad_kernel,
        out_shape=jax.ShapeDtypeStruct(shape, F32),
        grid_spec=pltpu.PrefetchScalarGridSpec(num_scalar_prefetch=1, grid=(steps,), in_specs=in_specs, out_specs=out_spec),
        compiler_params=pltpu.CompilerParams(vmem_limit_bytes=VMEM_LIMIT),
        cost_estimate=pl.CostEstimate(flops=2 * rows * shape[0] * shape[1], bytes_accessed=15 * 1024 * 1024, transcendentals=0),
    )(owner, *operands)


def wgrad_up(k, owner, acts, d_pre, grad_up):
    _, rows, width = acts.shape
    half, piece = width // 2, d_pre.shape[1] // PIECES
    steps = WGRAD_GRID
    un = piece // steps
    in_specs = [
        pl.BlockSpec((1, rows, half), lambda i, own: (0, 0, own[0])),
        pl.BlockSpec((rows, un), lambda i, own: (0, k * steps + i)),
        pl.BlockSpec((1, 1, half, un), lambda i, own: (0, 0, own[0], k * steps + i)),
    ]
    return wgrad_call(owner, (acts, d_pre, grad_up), in_specs, pl.BlockSpec((half, un), lambda i, own: (0, i)), (half, piece), steps)


def wgrad_down(k, owner, hid, g_own, grad_down):
    rows, width = g_own.shape
    piece = hid.shape[1] // 2 // PIECES
    steps = WGRAD_GRID
    vm = piece // steps
    in_specs = [
        pl.BlockSpec((rows, vm), lambda i, own: (0, (own[0] * PIECES + k) * steps + i)),
        pl.BlockSpec((rows, width), lambda i, own: (0, 0)),
        pl.BlockSpec((1, 1, vm, width), lambda i, own: (0, 0, (own[0] * PIECES + k) * steps + i, 0)),
    ]
    return wgrad_call(owner, (hid, g_own, grad_down), in_specs, pl.BlockSpec((vm, width), lambda i, own: (i, 0)), (piece, width), steps)


def update_kernel(n_pieces, n_alias, owner_ref, lr_ref, clip_ref, w_ref, m_ref, v_ref, *rest):
    g_refs = rest[:n_pieces]
    w_out, m_out, v_out = rest[n_pieces + n_alias:n_pieces + n_alias + 3]
    b_outs = rest[n_pieces + n_alias + 3:]
    clip, lr = clip_ref[0:1, 0:1], lr_ref[0]

    def run(g_ref, b_out):
        w = w_ref[0]
        q = clip * g_ref[...]
        m_new = BETA1 * m_ref[0] + (1.0 - BETA1) * q
        v_new = BETA2 * v_ref[0] + (1.0 - BETA2) * q * q
        m_hat = m_new * (1.0 / (1.0 - BETA1 ** ADAM_STEP))
        v_hat = v_new * (1.0 / (1.0 - BETA2 ** ADAM_STEP))
        w_new = w - lr * (m_hat / (jnp.sqrt(v_hat) + ADAM_EPS) + WEIGHT_DECAY * w)
        w_out[0], m_out[0], v_out[0] = w_new, m_new, v_new
        if b_out is not None:
            b_out[...] = w_new.astype(BF16)

    if n_pieces == 1:
        run(g_refs[0], b_outs[0] if b_outs else None)
    else:
        for p in range(n_pieces):
            pl.when(pl.program_id(0) == p)(functools.partial(run, g_refs[p], None))


def update_units(kind, first, owner, knobs, state, grads, chain, want_bf16):
    rows, cols = grads[0].shape
    n = len(grads)
    steps = UPDATE_GRID
    block = rows // steps
    if kind == 0:
        spec = pl.BlockSpec((1, block, cols), lambda p, i, own: (0, own[0] * steps + i, first + p))
    else:
        spec = pl.BlockSpec((1, block, cols), lambda p, i, own: (0, (own[0] * PIECES + first + p) * steps + i, 0))

    def piece_spec(q):
        return pl.BlockSpec((block, cols), lambda p, i, own: (jnp.clip((p - q) * steps + i, 0, steps - 1), 0))

    full = jax.ShapeDtypeStruct(state[0].shape, F32)
    out_shape, out_specs = (full,) * 3, (spec,) * 3
    if want_bf16:
        out_shape += (jax.ShapeDtypeStruct((rows, cols), BF16),)
        out_specs += (piece_spec(0),)
    size = n * rows * cols
    return pl.pallas_call(
        functools.partial(update_kernel, n, len(chain)),
        out_shape=out_shape,
        grid_spec=pltpu.PrefetchScalarGridSpec(
            num_scalar_prefetch=1,
            grid=(n, steps),
            in_specs=[pl.BlockSpec(memory_space=pltpu.SMEM), pl.BlockSpec(memory_space=pltpu.VMEM)] + [spec] * 3 + [piece_spec(q) for q in range(n)] + [ANY] * len(chain),
            out_specs=out_specs,
        ),
        input_output_aliases={6 + n + i: i for i in range(len(chain))},
        compiler_params=pltpu.CompilerParams(vmem_limit_bytes=UPDATE_VMEM),
        cost_estimate=pl.CostEstimate(flops=30 * size, bytes_accessed=28 * size, transcendentals=size),
    )(owner, *knobs, *state, *grads, *chain)


def norm_kernel(n_stages, n_rep, n_parts, *refs):
    parts, (max_ref, clip_ref, mine, slots, send_sem, recv_sem) = refs[:n_parts], refs[n_parts:]
    n_dev = n_stages * n_rep
    me = lax.axis_index("data") * n_stages + lax.axis_index("stage")
    total = parts[0][0]
    for part in parts[1:]:
        total = total + part[0]
    mine[...] = jnp.full(mine.shape, total, F32)
    slots[me] = jnp.full(mine.shape, total, F32)

    def place(d):
        q = lax.rem(me + d, n_dev)
        return {"data": q // n_stages, "stage": lax.rem(q, n_stages)}

    barrier = pltpu.get_barrier_semaphore()
    for d in range(1, n_dev):
        pl.semaphore_signal(barrier, inc=1, device_id=place(d), device_id_type=MESH_ID)
    pl.semaphore_wait(barrier, n_dev - 1)
    copies = []
    for d in range(1, n_dev):
        copies.append(pltpu.make_async_remote_copy(
            src_ref=mine, dst_ref=slots.at[me], send_sem=send_sem.at[d - 1], recv_sem=recv_sem.at[d - 1],
            device_id=place(d), device_id_type=MESH_ID))
        copies[-1].start()
    for copy in copies:
        copy.wait()
    square = slots[0]
    for q in range(1, n_dev):
        square = square + slots[q]
    clip_ref[...] = jnp.minimum(1.0, max_ref[0] / (jnp.sqrt(square) + NORM_EPS))


def clip_factor(n_stages, n_rep, parts, max_norm):
    n_dev = n_stages * n_rep
    return pl.pallas_call(
        functools.partial(norm_kernel, n_stages, n_rep, len(parts)),
        name="clip_factor",
        out_shape=jax.ShapeDtypeStruct((8, 128), F32),
        in_specs=[pl.BlockSpec(memory_space=pltpu.SMEM)] * (len(parts) + 1),
        out_specs=pl.BlockSpec(memory_space=pltpu.VMEM),
        scratch_shapes=[
            pltpu.VMEM((8, 128), F32),
            pltpu.VMEM((n_dev, 8, 128), F32),
            pltpu.SemaphoreType.DMA((n_dev - 1,)),
            pltpu.SemaphoreType.DMA((n_dev - 1,)),
        ],
        compiler_params=pltpu.CompilerParams(collective_id=2, has_side_effects=True),
        cost_estimate=pl.CostEstimate(flops=40000000, bytes_accessed=4096, transcendentals=0),
    )(*parts, max_norm)


def fwd_kernel(n_stages, n_rep, batch_ref, *refs):
    n_w = 2 * PIECES * n_rep
    w_refs = refs[:n_w]
    out_ref, up_ref, down_ref, x_buf, acc_ref, pre_buf, w_sem, recv_sem, send_sem = refs[n_w:]
    stage = lax.axis_index("stage")
    me = lax.axis_index("data")
    last = n_stages - 1
    n_chunks = x_buf.shape[0]
    hidden = up_ref.shape[1]
    n_tiles = hidden // FWD_TILE
    chunks_per_micro = n_chunks // batch_ref.shape[0]

    def batch_chunk(ref, c, lead):
        return ref.at[lead + (c // chunks_per_micro, span(lax.rem(c, chunks_per_micro), FWD_ROWS), slice(None))]

    copies = []
    for side in range(n_rep):
        owner = me if side == 0 else 1 - me
        for k in range(PIECES):
            u_src = w_refs[(2 * side) * PIECES + k]
            v_src = w_refs[(2 * side + 1) * PIECES + k]
            half_w, piece_n = u_src.shape
            piece_m = v_src.shape[0]
            u_dst = up_ref.at[span(owner, half_w), pl.ds(k * piece_n, piece_n)]
            v_dst = down_ref.at[span(owner * PIECES + k, piece_m), :]
            copies.append(pltpu.make_async_copy(u_src, u_dst, w_sem.at[len(copies)]))
            copies.append(pltpu.make_async_copy(v_src, v_dst, w_sem.at[len(copies)]))
    for copy in copies:
        copy.start()

    @pl.when(stage == 0)
    def _():
        def load(c, carry):
            pltpu.make_async_copy(batch_chunk(batch_ref, c, ()), x_buf.at[c], recv_sem.at[c]).start()
            return carry

        lax.fori_loop(0, n_chunks, load, 0)

    meet_neighbours(stage, n_stages)
    for copy in copies:
        copy.wait()

    def send_of(c):
        return pltpu.make_async_remote_copy(
            src_ref=batch_chunk(out_ref, c, (0,)), dst_ref=x_buf.at[c],
            send_sem=send_sem.at[c], recv_sem=recv_sem.at[c],
            device_id={"stage": stage + 1}, device_id_type=MESH_ID)

    def chunk(c, carry):
        pltpu.make_async_copy(batch_chunk(batch_ref, c, ()), x_buf.at[c], recv_sem.at[c]).wait()

        def products(j):
            pre_buf[j % 2] = dot_nn(x_buf[c], up_ref[:, pl.ds(j * FWD_TILE, FWD_TILE)])

        def rest(j):
            hid = gelu_value(pre_buf[j % 2]).astype(BF16)
            part = dot_nn(hid, down_ref[pl.ds(j * FWD_TILE, FWD_TILE), :])
            if j == 0:
                acc_ref[...] = x_buf[c].astype(F32) + part
            elif j < n_tiles - 1:
                acc_ref[...] += part
            else:
                out_ref[0, c // chunks_per_micro, span(lax.rem(c, chunks_per_micro), FWD_ROWS), :] = (acc_ref[...] + part).astype(BF16)

        products(0)
        for j in range(n_tiles):
            if j + 1 < n_tiles:
                products(j + 1)
            rest(j)

        @pl.when(stage < last)
        def _():
            send_of(c).start()

        return carry

    lax.fori_loop(0, n_chunks, chunk, 0)

    @pl.when(stage < last)
    def _():
        def finish(c, carry):
            send_of(c).wait_send()
            return carry

        lax.fori_loop(0, n_chunks, finish, 0)


def forward(n_stages, n_rep, next_batch, weights):
    n_micro, rows, width = next_batch.shape
    hidden = PIECES * weights[0].shape[1]
    n_chunks = n_micro * rows // FWD_ROWS
    return pl.pallas_call(
        functools.partial(fwd_kernel, n_stages, n_rep),
        name="forward",
        out_shape=pltpu.VMEM((1, n_micro, rows, width), BF16),
        in_specs=[ANY] * (1 + len(weights)),
        out_specs=pl.BlockSpec(memory_space=pltpu.VMEM),
        scratch_shapes=[
            pltpu.VMEM((width, hidden), BF16),
            pltpu.VMEM((hidden, width), BF16),
            pltpu.VMEM((n_chunks, FWD_ROWS, width), BF16),
            pltpu.VMEM((FWD_ROWS, width), F32),
            pltpu.VMEM((2, FWD_ROWS, FWD_TILE), F32),
            pltpu.SemaphoreType.DMA((len(weights),)),
            pltpu.SemaphoreType.DMA((n_chunks,)),
            pltpu.SemaphoreType.DMA((n_chunks,)),
        ],
        compiler_params=pltpu.CompilerParams(collective_id=1, has_side_effects=True, vmem_limit_bytes=FWD_VMEM),
        cost_estimate=pl.CostEstimate(flops=4 * n_micro * rows * width * hidden, bytes_accessed=6 * rows * hidden, transcendentals=n_micro * rows * hidden),
    )(next_batch, *weights)


def store_kernel(y_ref, out_ref, sem):
    copies = []
    for i in range(y_ref.shape[1]):
        copies.append(pltpu.make_async_copy(y_ref.at[0, i], out_ref.at[0, i], sem.at[i]))
        copies[-1].start()
    for copy in copies:
        copy.wait()


def store(y):
    return pl.pallas_call(
        store_kernel,
        name="store",
        out_shape=jax.ShapeDtypeStruct(y.shape, y.dtype),
        in_specs=[pl.BlockSpec(memory_space=pltpu.VMEM)],
        out_specs=ANY,
        scratch_shapes=[pltpu.SemaphoreType.DMA((y.shape[1],))],
        compiler_params=pltpu.CompilerParams(vmem_limit_bytes=STORE_VMEM),
        cost_estimate=pl.CostEstimate(flops=4000000, bytes_accessed=2 * y.size, transcendentals=0),
    )(y)


def solution(mesh):
    n_stages = mesh.shape["stage"]
    n_rep = mesh.shape["data"]
    swap = [(i, n_rep - 1 - i) for i in range(n_rep)]

    def exchange(x):
        return lax.ppermute(x, "data", swap)

    def local_step(master_up, master_down, mom1_up, mom1_down, mom2_up, mom2_down, grad_up, grad_down, stage_acts, loss_grad, next_batch, learn_rate, max_norm):
        me = lax.axis_index("data")
        mine = jnp.reshape(me, (1,)).astype(jnp.int32)
        other = 1 - mine
        hid, d_pre, g_own = backward(n_stages, stage_acts, loss_grad, master_up, master_down)

        units = [(kind, k) for k in range(PIECES) for kind in (0, 1)]

        def wgrad(unit, owner):
            if unit[0] == 0:
                return wgrad_up(unit[1], owner, stage_acts, d_pre, grad_up)
            return wgrad_down(unit[1], owner, hid, g_own, grad_down)

        arrived, whose = {}, other
        for unit in units:
            part = wgrad(unit, whose)
            arrived[unit] = exchange(part)
            whose = lax.optimization_barrier((other, part))[0]
        gbar, squares = {}, []
        for unit in units:
            gbar[unit] = (wgrad(unit, mine) + arrived[unit]) * (1.0 / n_rep)
            squares.append(jnp.reshape(jnp.sum(gbar[unit] * gbar[unit]), (1,)))
        clip = clip_factor(n_stages, n_rep, squares, jnp.reshape(max_norm, (1,)))
        knobs = (jnp.reshape(learn_rate, (1,)), clip)
        gbar_other = {}
        for unit in F32_FIRST:
            gbar_other[unit] = exchange(lax.optimization_barrier((gbar[unit], clip))[0])
        state = ((master_up, mom1_up, mom2_up), (master_down, mom1_down, mom2_down))
        chain = [(), ()]

        def update(unit, owner, grad):
            res = update_units(unit[0], unit[1], owner, knobs, state[unit[0]], [grad], chain[unit[0]], True)
            chain[unit[0]] = res[:3]
            return res[3]

        def update_group(kind, first, stop):
            grads = [gbar_other[kind, k] for k in range(first, stop)]
            chain[kind] = update_units(kind, first, other, knobs, state[kind], grads, chain[kind], False)

        late = [unit for unit in units if unit not in F32_FIRST]
        own_w, other_w = {}, {}
        for unit in late + list(F32_FIRST):
            own_w[unit] = update(unit, mine, gbar[unit])
            if unit in late:
                other_w[unit] = exchange(own_w[unit])
        for unit in late:
            ready = lax.optimization_barrier((gbar[unit], own_w[late[-1]]))[0]
            gbar_other[unit] = exchange(ready)
        for unit in F32_FIRST:
            other_w[unit] = update(unit, other, gbar_other[unit])
        weights = []
        for side in (own_w, other_w):
            for kind in (0, 1):
                weights += [side[kind, k] for k in range(PIECES)]
        stage_outs = store(forward(n_stages, n_rep, next_batch, weights))
        for kind, first, stop in TAIL:
            update_group(kind, first, stop)
        (new_up, new_m1_up, new_m2_up), (new_down, new_m1_down, new_m2_down) = chain
        return (new_up, new_down, new_m1_up, new_m1_down, new_m2_up, new_m2_down, stage_outs)

    w_spec = P("stage", None, None)
    g_spec = P("data", "stage", None, None)
    in_specs = (w_spec,) * 6 + (g_spec, g_spec, P("stage", "data", None), P("data", None), P(None, "data", None), P(), P())
    out_specs = (w_spec,) * 6 + (P("stage", None, "data", None),)
    return jax.shard_map(local_step, mesh=mesh, in_specs=in_specs, out_specs=out_specs, check_vma=False)
```

profile of v0, /device:TPU:3, one launch (start us, length us, event | category | flops | bytes accessed | tf_op | source)
XLA Modules:
  0.0 842.8 jit_solution(1159621817052109103)
XLA Ops:
  0.6 78.5 %backward.1 = (bf16[4096,3072]{1,0:T(8,128)(2,1)}, bf16[4096,3072]{1,0:T(8,128)(2,1)}, bf16[4096,768]{1,0:T(8,128)(2,1)}) custom-call(bf16[1,4096,768]{2,1,0:T(8,128)(2,1)} %left_ref.23, bf16[4096,768]{1,0:T(8,128)(2,1)} %dy_ref.1, f32[1,768,3072]{2,1,0:T(8,128)} %w_ref.31, f32[1,3072,768]{2,1,0:T(8,128)} %w_ref.33), custom_call_target="tpu_custom_call" | custom-call | flops 57982058496 | bytes 75497472 | tf_op jit(solution)/shard_map/backward/pallas_call | solution.py:223
  139.9 7.4 shard_map.186
  154.3 7.4 shard_map.190
  168.8 7.4 shard_map.194
  183.1 7.4 shard_map.198
  190.6 7.4 shard_map.191
  204.9 7.5 shard_map.195
  226.2 7.4 shard_map.199
  233.7 7.5 shard_map.202
  249.4 7.6 shard_map.203
  282.1 15.0 %collective-permute-done.7 = f32[256,768]{1,0:T(8,128)S(1)} collective-permute-done((f32[256,768]{1,0:T(8,128)}, f32[256,768]{1,0:T(8,128)S(1)}, u32[]{:S(2)}, u32[]{:S(2)}) %collective-permute-start.7) | collective-permute-done | bytes 786464 | tf_op jit(solution)/shard_map/ppermute | solution.py:553
  298.7 15.2 %collective-permute-done.8 = f32[384,512]{1,0:T(8,128)S(1)} collective-permute-done((f32[384,512]{1,0:T(8,128)S(1)}, f32[384,512]{1,0:T(8,128)S(1)}, u32[]{:S(2)}, u32[]{:S(2)}) %collective-permute-start.8) | collective-permute-done | bytes 786464 | tf_op jit(solution)/shard_map/ppermute | solution.py:553
  315.7 15.0 %collective-permute-done.9 = f32[256,768]{1,0:T(8,128)S(1)} collective-permute-done((f32[256,768]{1,0:T(8,128)S(1)}, f32[256,768]{1,0:T(8,128)S(1)}, u32[]{:S(2)}, u32[]{:S(2)}) %collective-permute-start.9) | collective-permute-done | bytes 786464 | tf_op jit(solution)/shard_map/ppermute | solution.py:553
  332.4 15.2 %collective-permute-done.10 = f32[384,512]{1,0:T(8,128)S(1)} collective-permute-done((f32[384,512]{1,0:T(8,128)S(1)}, f32[384,512]{1,0:T(8,128)S(1)}, u32[]{:S(2)}, u32[]{:S(2)}) %collective-permute-start.10) | collective-permute-done | bytes 786464 | tf_op jit(solution)/shard_map/ppermute | solution.py:553
  349.4 15.1 %collective-permute-done.11 = f32[256,768]{1,0:T(8,128)S(1)} collective-permute-done((f32[256,768]{1,0:T(8,128)S(1)}, f32[256,768]{1,0:T(8,128)S(1)}, u32[]{:S(2)}, u32[]{:S(2)}) %collective-permute-start.11) | collective-permute-done | bytes 786464 | tf_op jit(solution)/shard_map/ppermute | solution.py:553
  366.1 43.9 %clip_factor.1.clip_ref = f32[8,128]{1,0:T(8,128)} custom-call(f32[1]{0:T(128)} %bitcast.2.refs_0_, f32[1]{0:T(128)} %bitcast.3.refs_1_, f32[1]{0:T(128)} %bitcast.4.refs_2_, f32[1]{0:T(128)} %bitcast.5.refs_3_, f32[1]{0:T(128)} %bitcast.6.refs_4_, f32[1]{0:T(128)} %bitcast.7.refs_5_, f32[1]{0:T(128)} %bitcast.8.refs_6_, f32[1]{0:T(128)} %bitcast.9.refs_7_, ...), custom_call_target="tpu_custom_call" | custom-call | flops 40000000 | bytes 4096 | tf_op jit(solution)/shard_map/clip_factor/pallas_call | solution.py:396
  490.7 40.9 %collective-permute-done.32.refs_21_ = bf16[256,768]{1,0:T(8,128)(2,1)S(1)} collective-permute-done((bf16[256,768]{1,0:T(8,128)(2,1)}, bf16[256,768]{1,0:T(8,128)(2,1)S(1)}, u32[]{:S(2)}, u32[]{:S(2)}) %collective-permute-start.32) | collective-permute-done | bytes 393248 | tf_op jit(solution)/shard_map/ppermute | solution.py:553
  566.7 15.6 %collective-permute-done.14.rest_1_ = f32[384,512]{1,0:T(8,128)} collective-permute-done((f32[384,512]{1,0:T(8,128)S(1)}, f32[384,512]{1,0:T(8,128)}, u32[]{:S(2)}, u32[]{:S(2)}) %collective-permute-start.14) | collective-permute-done | bytes 786464 | tf_op jit(solution)/shard_map/ppermute | solution.py:553
  583.5 15.6 %collective-permute-done.15.rest_2_ = f32[384,512]{1,0:T(8,128)} collective-permute-done((f32[384,512]{1,0:T(8,128)S(1)}, f32[384,512]{1,0:T(8,128)}, u32[]{:S(2)}, u32[]{:S(2)}) %collective-permute-start.15) | collective-permute-done | bytes 786464 | tf_op jit(solution)/shard_map/ppermute | solution.py:553
  600.4 15.5 %collective-permute-done.16.rest_3_ = f32[384,512]{1,0:T(8,128)S(1)} collective-permute-done((f32[384,512]{1,0:T(8,128)S(1)}, f32[384,512]{1,0:T(8,128)S(1)}, u32[]{:S(2)}, u32[]{:S(2)}) %collective-permute-start.16) | collective-permute-done | bytes 786464 | tf_op jit(solution)/shard_map/ppermute | solution.py:553
  617.1 15.6 %collective-permute-done.19.rest_0_ = f32[256,768]{1,0:T(8,128)S(1)} collective-permute-done((f32[256,768]{1,0:T(8,128)}, f32[256,768]{1,0:T(8,128)S(1)}, u32[]{:S(2)}, u32[]{:S(2)}) %collective-permute-start.19) | collective-permute-done | bytes 786464 | tf_op jit(solution)/shard_map/ppermute | solution.py:553
  634.0 161.1 %forward.1.y_ref = bf16[1,2,4096,768]{3,2,1,0:T(8,128)(2,1)S(1)} custom-call(bf16[2,4096,768]{2,1,0:T(8,128)(2,1)} %batch_ref.1, bf16[384,512]{1,0:T(8,128)(2,1)} %get-tuple-element.175.refs_0_, bf16[384,512]{1,0:T(8,128)(2,1)} %get-tuple-element.176.refs_1_, bf16[384,512]{1,0:T(8,128)(2,1)} %get-tuple-element.177.refs_2_, ...), custom_call_target="tpu_custom_call" | custom-call | flops 77309411328 | bytes 75497472 | tf_op jit(solution)/shard_map/forward/pallas_call | solution.py:504
  799.9 15.3 %shard_map.217 = (f32[1,768,3072]{2,1,0:T(8,128)}, f32[1,768,3072]{2,1,0:T(8,128)}, f32[1,768,3072]{2,1,0:T(8,128)}) custom-call(s32[1]{0:T(128)S(6)} %sub.3.owner_ref, f32[1]{0:T(128)} %bitcast.28.lr_ref, f32[8,128]{1,0:T(8,128)} %clip_factor.1.clip_ref, f32[1,768,3072]{2,1,0:T(8,128)} %w_ref.31, ...), custom_call_target="tpu_custom_call", output_to_operand_aliasing={{0}: (10, {}), {1}: (11, {}), {2}: (12, {})} | custom-call | flops 23592960 | bytes 22020096 | tf_op jit(solution)/shard_map/pallas_call | solution.py:347
  819.7 18.7 %shard_map.219 = (f32[1,3072,768]{2,1,0:T(8,128)}, f32[1,3072,768]{2,1,0:T(8,128)}, f32[1,3072,768]{2,1,0:T(8,128)}) custom-call(s32[1]{0:T(128)S(6)} %sub.3.owner_ref, f32[1]{0:T(128)} %bitcast.30.lr_ref, f32[8,128]{1,0:T(8,128)} %clip_factor.1.clip_ref, f32[1,3072,768]{2,1,0:T(8,128)} %w_ref.33, ...), custom_call_target="tpu_custom_call", output_to_operand_aliasing={{0}: (11, {}), {1}: (12, {}), {2}: (13, {})} | custom-call | flops 29491200 | bytes 27525120 | tf_op jit(solution)/shard_map/pallas_call | solution.py:347
  (165 shorter events, 277.2 us)
Async XLA Ops:
  86.0 171.1 %collective-permute-start = (f32[384,512]{1,0:T(8,128)}, f32[384,512]{1,0:T(8,128)}, u32[]{:S(2)}, u32[]{:S(2)}) collective-permute-start(f32[384,512]{1,0:T(8,128)} %shard_map.181), channel_id=1, source_target_pairs={{0,4},{4,0},{1,5},{5,1},{2,6},{6,2},{3,7},{7,3}} | collective-permute-start | bytes 2359304 | tf_op jit(solution)/shard_map/ppermute | solution.py:553
  94.7 165.6 %collective-permute-start.1 = (f32[256,768]{1,0:T(8,128)}, f32[256,768]{1,0:T(8,128)}, u32[]{:S(2)}, u32[]{:S(2)}) collective-permute-start(f32[256,768]{1,0:T(8,128)} %shard_map.183), channel_id=1, source_target_pairs={{0,4},{4,0},{1,5},{5,1},{2,6},{6,2},{3,7},{7,3}} | collective-permute-start | bytes 2359304 | tf_op jit(solution)/shard_map/ppermute | solution.py:553
  101.7 162.9 %collective-permute-start.2 = (f32[384,512]{1,0:T(8,128)}, f32[384,512]{1,0:T(8,128)}, u32[]{:S(2)}, u32[]{:S(2)}) collective-permute-start(f32[384,512]{1,0:T(8,128)} %shard_map.185), channel_id=1, source_target_pairs={{0,4},{4,0},{1,5},{5,1},{2,6},{6,2},{3,7},{7,3}} | collective-permute-start | bytes 2359304 | tf_op jit(solution)/shard_map/ppermute | solution.py:553
  110.4 157.2 %collective-permute-start.3 = (f32[256,768]{1,0:T(8,128)}, f32[256,768]{1,0:T(8,128)}, u32[]{:S(2)}, u32[]{:S(2)}) collective-permute-start(f32[256,768]{1,0:T(8,128)} %shard_map.187), channel_id=1, source_target_pairs={{0,4},{4,0},{1,5},{5,1},{2,6},{6,2},{3,7},{7,3}} | collective-permute-start | bytes 2359304 | tf_op jit(solution)/shard_map/ppermute | solution.py:553
  117.5 154.2 %collective-permute-start.4 = (f32[384,512]{1,0:T(8,128)}, f32[384,512]{1,0:T(8,128)}, u32[]{:S(2)}, u32[]{:S(2)}) collective-permute-start(f32[384,512]{1,0:T(8,128)} %shard_map.189), channel_id=1, source_target_pairs={{0,4},{4,0},{1,5},{5,1},{2,6},{6,2},{3,7},{7,3}} | collective-permute-start | bytes 2359304 | tf_op jit(solution)/shard_map/ppermute | solution.py:553
  267.6 46.3 %collective-permute-start.8 = (f32[384,512]{1,0:T(8,128)S(1)}, f32[384,512]{1,0:T(8,128)S(1)}, u32[]{:S(2)}, u32[]{:S(2)}) collective-permute-start(f32[384,512]{1,0:T(8,128)S(1)} %copy-done.24), channel_id=1, source_target_pairs={{0,4},{4,0},{1,5},{5,1},{2,6},{6,2},{3,7},{7,3}} | collective-permute-start | bytes 2359304 | tf_op jit(solution)/shard_map/ppermute | solution.py:553
  271.7 59.0 %collective-permute-start.9 = (f32[256,768]{1,0:T(8,128)S(1)}, f32[256,768]{1,0:T(8,128)S(1)}, u32[]{:S(2)}, u32[]{:S(2)}) collective-permute-start(f32[256,768]{1,0:T(8,128)S(1)} %copy-done.23), channel_id=1, source_target_pairs={{0,4},{4,0},{1,5},{5,1},{2,6},{6,2},{3,7},{7,3}} | collective-permute-start | bytes 2359304 | tf_op jit(solution)/shard_map/ppermute | solution.py:553
  274.7 72.9 %collective-permute-start.10 = (f32[384,512]{1,0:T(8,128)S(1)}, f32[384,512]{1,0:T(8,128)S(1)}, u32[]{:S(2)}, u32[]{:S(2)}) collective-permute-start(f32[384,512]{1,0:T(8,128)S(1)} %copy-done.22), channel_id=1, source_target_pairs={{0,4},{4,0},{1,5},{5,1},{2,6},{6,2},{3,7},{7,3}} | collective-permute-start | bytes 2359304 | tf_op jit(solution)/shard_map/ppermute | solution.py:553
  280.2 84.3 %collective-permute-start.11 = (f32[256,768]{1,0:T(8,128)S(1)}, f32[256,768]{1,0:T(8,128)S(1)}, u32[]{:S(2)}, u32[]{:S(2)}) collective-permute-start(f32[256,768]{1,0:T(8,128)S(1)} %copy-done.21), channel_id=1, source_target_pairs={{0,4},{4,0},{1,5},{5,1},{2,6},{6,2},{3,7},{7,3}} | collective-permute-start | bytes 2359304 | tf_op jit(solution)/shard_map/ppermute | solution.py:553
  414.6 49.0 %collective-permute-start.24 = (bf16[384,512]{1,0:T(8,128)(2,1)}, bf16[384,512]{1,0:T(8,128)(2,1)}, u32[]{:S(2)}, u32[]{:S(2)}) collective-permute-start(bf16[384,512]{1,0:T(8,128)(2,1)} %get-tuple-element.176.refs_1_), channel_id=1, source_target_pairs={{0,4},{4,0},{1,5},{5,1},{2,6},{6,2},{3,7},{7,3}} | collective-permute-start | bytes 1179656 | tf_op jit(solution)/shard_map/ppermute | solution.py:553
  419.4 45.4 %collective-permute-start.25 = (bf16[384,512]{1,0:T(8,128)(2,1)}, bf16[384,512]{1,0:T(8,128)(2,1)}, u32[]{:S(2)}, u32[]{:S(2)}) collective-permute-start(bf16[384,512]{1,0:T(8,128)(2,1)} %get-tuple-element.177.refs_2_), channel_id=1, source_target_pairs={{0,4},{4,0},{1,5},{5,1},{2,6},{6,2},{3,7},{7,3}} | collective-permute-start | bytes 1179656 | tf_op jit(solution)/shard_map/ppermute | solution.py:553
  466.3 83.4 %collective-permute-start.12 = (f32[384,512]{1,0:T(8,128)S(1)}, f32[384,512]{1,0:T(8,128)S(1)}, u32[]{:S(2)}, u32[]{:S(2)}) collective-permute-start(f32[384,512]{1,0:T(8,128)S(1)} %copy-done.4), channel_id=1, source_target_pairs={{0,4},{4,0},{1,5},{5,1},{2,6},{6,2},{3,7},{7,3}} | collective-permute-start | bytes 2359304 | tf_op jit(solution)/shard_map/ppermute | solution.py:553
  466.5 83.5 %collective-permute-start.17 = (f32[384,512]{1,0:T(8,128)S(1)}, f32[384,512]{1,0:T(8,128)S(1)}, u32[]{:S(2)}, u32[]{:S(2)}) collective-permute-start(f32[384,512]{1,0:T(8,128)S(1)} %copy-done), channel_id=1, source_target_pairs={{0,4},{4,0},{1,5},{5,1},{2,6},{6,2},{3,7},{7,3}} | collective-permute-start | bytes 2359304 | tf_op jit(solution)/shard_map/ppermute | solution.py:553
  472.7 59.0 %collective-permute-start.32 = (bf16[256,768]{1,0:T(8,128)(2,1)}, bf16[256,768]{1,0:T(8,128)(2,1)S(1)}, u32[]{:S(2)}, u32[]{:S(2)}) collective-permute-start(bf16[256,768]{1,0:T(8,128)(2,1)} %get-tuple-element.184.refs_9_), channel_id=1, source_target_pairs={{0,4},{4,0},{1,5},{5,1},{2,6},{6,2},{3,7},{7,3}} | collective-permute-start | bytes 1179656 | tf_op jit(solution)/shard_map/ppermute | solution.py:553
  481.1 59.0 %collective-permute-start.33 = (bf16[256,768]{1,0:T(8,128)(2,1)}, bf16[256,768]{1,0:T(8,128)(2,1)S(1)}, u32[]{:S(2)}, u32[]{:S(2)}) collective-permute-start(bf16[256,768]{1,0:T(8,128)(2,1)} %get-tuple-element.185.refs_10_), channel_id=1, source_target_pairs={{0,4},{4,0},{1,5},{5,1},{2,6},{6,2},{3,7},{7,3}} | collective-permute-start | bytes 1179656 | tf_op jit(solution)/shard_map/ppermute | solution.py:553
  489.5 59.0 %collective-permute-start.34 = (bf16[256,768]{1,0:T(8,128)(2,1)}, bf16[256,768]{1,0:T(8,128)(2,1)S(1)}, u32[]{:S(2)}, u32[]{:S(2)}) collective-permute-start(bf16[256,768]{1,0:T(8,128)(2,1)} %get-tuple-element.126.refs_11_), channel_id=1, source_target_pairs={{0,4},{4,0},{1,5},{5,1},{2,6},{6,2},{3,7},{7,3}} | collective-permute-start | bytes 1179656 | tf_op jit(solution)/shard_map/ppermute | solution.py:553
  548.5 50.7 %collective-permute-start.15 = (f32[384,512]{1,0:T(8,128)S(1)}, f32[384,512]{1,0:T(8,128)}, u32[]{:S(2)}, u32[]{:S(2)}) collective-permute-start(f32[384,512]{1,0:T(8,128)S(1)} %copy-done.2), channel_id=1, source_target_pairs={{0,4},{4,0},{1,5},{5,1},{2,6},{6,2},{3,7},{7,3}} | collective-permute-start | bytes 2359304 | tf_op jit(solution)/shard_map/ppermute | solution.py:553
  549.7 66.2 %collective-permute-start.16 = (f32[384,512]{1,0:T(8,128)S(1)}, f32[384,512]{1,0:T(8,128)S(1)}, u32[]{:S(2)}, u32[]{:S(2)}) collective-permute-start(f32[384,512]{1,0:T(8,128)S(1)} %copy-done.3), channel_id=1, source_target_pairs={{0,4},{4,0},{1,5},{5,1},{2,6},{6,2},{3,7},{7,3}} | collective-permute-start | bytes 2359304 | tf_op jit(solution)/shard_map/ppermute | solution.py:553
  550.6 82.1 %collective-permute-start.19 = (f32[256,768]{1,0:T(8,128)}, f32[256,768]{1,0:T(8,128)S(1)}, u32[]{:S(2)}, u32[]{:S(2)}) collective-permute-start(f32[256,768]{1,0:T(8,128)} %get-tuple-element.159.rest_0_), channel_id=1, source_target_pairs={{0,4},{4,0},{1,5},{5,1},{2,6},{6,2},{3,7},{7,3}} | collective-permute-start | bytes 2359304 | tf_op jit(solution)/shard_map/ppermute | solution.py:553
  565.5 272.9 %collective-permute-start.18 = (f32[256,768]{1,0:T(8,128)}, f32[256,768]{1,0:T(8,128)}, u32[]{:S(2)}, u32[]{:S(2)}) collective-permute-start(f32[256,768]{1,0:T(8,128)} %get-tuple-element.158.rest_0_), channel_id=1, source_target_pairs={{0,4},{4,0},{1,5},{5,1},{2,6},{6,2},{3,7},{7,3}} | collective-permute-start | bytes 2359304 | tf_op jit(solution)/shard_map/ppermute | solution.py:553
  582.3 237.3 %collective-permute-start.20 = (f32[256,768]{1,0:T(8,128)}, f32[256,768]{1,0:T(8,128)}, u32[]{:S(2)}, u32[]{:S(2)}) collective-permute-start(f32[256,768]{1,0:T(8,128)} %get-tuple-element.160.rest_0_), channel_id=1, source_target_pairs={{0,4},{4,0},{1,5},{5,1},{2,6},{6,2},{3,7},{7,3}} | collective-permute-start | bytes 2359304 | tf_op jit(solution)/shard_map/ppermute | solution.py:553
  599.2 220.5 %collective-permute-start.21 = (f32[256,768]{1,0:T(8,128)}, f32[256,768]{1,0:T(8,128)}, u32[]{:S(2)}, u32[]{:S(2)}) collective-permute-start(f32[256,768]{1,0:T(8,128)} %get-tuple-element.161.rest_0_), channel_id=1, source_target_pairs={{0,4},{4,0},{1,5},{5,1},{2,6},{6,2},{3,7},{7,3}} | collective-permute-start | bytes 2359304 | tf_op jit(solution)/shard_map/ppermute | solution.py:553
  615.9 203.7 %collective-permute-start.22 = (f32[256,768]{1,0:T(8,128)}, f32[256,768]{1,0:T(8,128)}, u32[]{:S(2)}, u32[]{:S(2)}) collective-permute-start(f32[256,768]{1,0:T(8,128)} %get-tuple-element.162.rest_0_), channel_id=1, source_target_pairs={{0,4},{4,0},{1,5},{5,1},{2,6},{6,2},{3,7},{7,3}} | collective-permute-start | bytes 2359304 | tf_op jit(solution)/shard_map/ppermute | solution.py:553
  632.8 186.9 %collective-permute-start.23 = (f32[256,768]{1,0:T(8,128)}, f32[256,768]{1,0:T(8,128)}, u32[]{:S(2)}, u32[]{:S(2)}) collective-permute-start(f32[256,768]{1,0:T(8,128)} %get-tuple-element.163.rest_0_), channel_id=1, source_target_pairs={{0,4},{4,0},{1,5},{5,1},{2,6},{6,2},{3,7},{7,3}} | collective-permute-start | bytes 2359304 | tf_op jit(solution)/shard_map/ppermute | solution.py:553
  (42 other events, 1381.6 us)
where the time goes:
time: 845 us; the launch traced here: 843 us
  Pallas kernels  563 us (67%)
  waiting for transfers between devices  220 us (26%)
  starting transfers between devices  30.8 us (4%)
  other arithmetic  26 us (3%)
    ppermute x35, waiting for transfers between devices, exchange(): return lax.ppermute(x, 'data', swap)  220 us
    pallas_call x24, Pallas kernels, wgrad_call(): pl.pallas_call(wgrad_kernel, out_shape=jax.ShapeDtypeStruct(shape, F32),...  172 us
    pallas_call x1, Pallas kernels, forward(): pl.pallas_call(functools.partial(fwd_kernel, n_stages, n_rep), name='forw...  161 us
    pallas_call x17, Pallas kernels, update_units(): pl.pallas_call(functools.partial(update_kernel, n, len(chain)), out_shape...  102 us
    pallas_call x1, Pallas kernels, backward(): pl.pallas_call(functools.partial(back_kernel, n_stages), name='backward',...  78.5 us
    pallas_call x1, Pallas kernels, clip_factor(): pl.pallas_call(functools.partial(norm_kernel, n_stages, n_rep, len(parts)...  43.9 us
    ppermute x35, starting transfers between devices, exchange(): return lax.ppermute(x, 'data', swap)  30.8 us
    reduce_sum x12, other arithmetic, local_step(): squares.append(jnp.reshape(jnp.sum(gbar[unit] * gbar[unit]), (1,)))  26 us
  transfers between devices with their start and end apart: 35, of which 17 were waited for; matrix products, arithmetic and copies ran while one was open for 3% of the time, Pallas kernels for 50%

commit v1 on v0

--- a/solution.py
+++ b/solution.py
@@ -23,11 +23,11 @@
 FWD_TILE = 512
 PIECES = 6
 F32_FIRST = ((0, 0),)
-TAIL = ((0, 1, 5), (1, 0, 5), (0, 5, 6), (1, 5, 6))
-STAGING = 4
-WGRAD_STEP = 1024
-WGRAD_GRID = 2
-UPDATE_GRID = 4
+GROUPS = ((0, 0, 1), (1, 0, 2), (0, 1, 2), (1, 2, 2), (0, 3, 2), (1, 4, 2), (0, 5, 1))
+TAIL = ((1, 0, 4), (0, 1, 5), (1, 4, 6), (0, 5, 6))
+STAGING = 3
+WGRAD_STEP = 4096
+SLAB = 32
 
 BF16 = jnp.bfloat16
 F32 = jnp.float32
@@ -87,56 +87,61 @@
 
 
 def back_kernel(n_stages, acts_ref, dy_ref, up32_ref, down32_ref, hid_ref, dpre_ref, gown_ref,
-                up_ref, down_ref, g_buf, h_buf, p_buf, dx_buf, acc_ref, pre_buf, dh_buf, stage_u, stage_v,
-                u_sem, v_sem, recv_sem, send_sem, gown_sem, h_sem, p_sem):
+                up_ref, down_ref, a_buf, g_buf, h_buf, p_buf, dx_buf, acc_ref, pre_buf, dh_buf, stage_u, stage_v,
+                u_sem, v_sem, a_sem, recv_sem, send_sem, gown_sem, h_sem, p_sem):
     stage = lax.axis_index("stage")
     last = n_stages - 1
-    rows_all, width = g_buf.shape
+    rows_all = g_buf.shape[0]
     hidden = up_ref.shape[1]
     n_chunks = rows_all // BACK_ROWS
     n_tiles = hidden // BACK_TILE
-    u_rows = stage_u.shape[1]
-    v_rows = stage_v.shape[1]
-    n_cast = width // u_rows
-
-    def u_copy(i, slot):
-        return pltpu.make_async_copy(up32_ref.at[0, span(i, u_rows), :], stage_u.at[slot], u_sem.at[slot])
-
-    def v_copy(i, slot):
-        return pltpu.make_async_copy(down32_ref.at[0, span(i, v_rows), :], stage_v.at[slot], v_sem.at[slot])
-
-    for i in range(STAGING):
-        u_copy(i, i).start()
-        v_copy(i, i).start()
+
+    def tile_copies(j):
+        slot, cols = j % STAGING, pl.ds(j * BACK_TILE, BACK_TILE)
+        return (pltpu.make_async_copy(up32_ref.at[0, :, cols], stage_u.at[slot], u_sem.at[slot]),
+                pltpu.make_async_copy(down32_ref.at[0, cols, :], stage_v.at[slot], v_sem.at[slot]))
 
     def rows_of(c):
-        return span(c, BACK_ROWS)
+        return pl.ds(c * BACK_ROWS, BACK_ROWS) if isinstance(c, int) else span(c, BACK_ROWS)
+
+    def a_copy(c):
+        return pltpu.make_async_copy(acts_ref.at[0, rows_of(c), :], a_buf.at[rows_of(c), :], a_sem.at[c])
+
+    def dy_copy(c):
+        return pltpu.make_async_copy(dy_ref.at[rows_of(c), :], g_buf.at[rows_of(c), :], recv_sem.at[c])
+
+    a_copy(0).start()
 
     @pl.when(stage == last)
     def _():
-        def load(c, carry):
-            pltpu.make_async_copy(dy_ref.at[rows_of(c), :], g_buf.at[rows_of(c), :], recv_sem.at[c]).start()
-            return carry
-
-        lax.fori_loop(0, n_chunks, load, 0)
+        dy_copy(0).start()
+
+    for j in range(STAGING):
+        for copy in tile_copies(j):
+            copy.start()
+
+    def load_rest(c, carry):
+        a_copy(c).start()
+
+        @pl.when(stage == last)
+        def _():
+            dy_copy(c).start()
+
+        return carry
+
+    def cast_tile(j):
+        cols = pl.ds(j * BACK_TILE, BACK_TILE)
+        for copy in tile_copies(j):
+            copy.wait()
+        up_ref[:, cols] = stage_u[j % STAGING].astype(BF16)
+        down_ref[cols, :] = stage_v[j % STAGING].astype(BF16)
+        if j + STAGING < n_tiles:
+            for copy in tile_copies(j + STAGING):
+                copy.start()
+        if j == n_tiles - STAGING:
+            lax.fori_loop(1, n_chunks, load_rest, 0)
 
     meet_neighbours(stage, n_stages)
-
-    def cast(i, carry):
-        slot = lax.rem(i, STAGING)
-        u_copy(i, slot).wait()
-        up_ref[span(i, u_rows), :] = stage_u[slot].astype(BF16)
-        v_copy(i, slot).wait()
-        down_ref[span(i, v_rows), :] = stage_v[slot].astype(BF16)
-
-        @pl.when(i + STAGING < n_cast)
-        def _():
-            u_copy(i + STAGING, slot).start()
-            v_copy(i + STAGING, slot).start()
-
-        return carry
-
-    lax.fori_loop(0, n_cast, cast, 0)
 
     def send_of(c):
         return pltpu.make_async_remote_copy(
@@ -151,21 +156,24 @@
     def gown_copy(c):
         return pltpu.make_async_copy(g_buf.at[rows_of(c), :], gown_ref.at[rows_of(c), :], gown_sem.at[c])
 
-    def chunk(c, carry):
-        slot = lax.rem(c, 2)
+    def chunk(c, carry, casting=False):
+        slot = c % 2 if casting else lax.rem(c, 2)
         rows = rows_of(c)
-
-        @pl.when(c >= 2)
-        def _():
-            for copy in out_copies(c - 2, slot):
-                copy.wait()
-
-        pltpu.make_async_copy(dy_ref.at[rows, :], g_buf.at[rows, :], recv_sem.at[c]).wait()
+        if not casting:
+            @pl.when(c >= 2)
+            def _():
+                for copy in out_copies(c - 2, slot):
+                    copy.wait()
+
+        a_copy(c).wait()
+        dy_copy(c).wait()
         gown_copy(c).start()
 
         def products(j):
+            if casting:
+                cast_tile(j)
             cols = pl.ds(j * BACK_TILE, BACK_TILE)
-            pre_buf[j % 2] = dot_nn(acts_ref[0, rows, :], up_ref[:, cols])
+            pre_buf[j % 2] = dot_nn(a_buf[rows, :], up_ref[:, cols])
             dh_buf[j % 2] = dot_nt(g_buf[rows, :], down_ref[cols, :])
 
         def rest(j):
@@ -196,7 +204,16 @@
 
         return carry
 
-    lax.fori_loop(0, n_chunks, chunk, 0)
+    @pl.when(stage == last)
+    def _():
+        chunk(0, 0, casting=True)
+
+    @pl.when(stage < last)
+    def _():
+        for j in range(n_tiles):
+            cast_tile(j)
+
+    lax.fori_loop(stage // last, n_chunks, chunk, 0)
 
     for c in (n_chunks - 2, n_chunks - 1):
         for copy in out_copies(c, c % 2):
@@ -218,17 +235,17 @@
     _, rows, width = acts.shape
     hidden = up32.shape[2]
     n_chunks = rows // BACK_ROWS
-    u_rows, v_rows = width // 12, hidden // 12
     wide = jax.ShapeDtypeStruct((rows, hidden), BF16)
     return pl.pallas_call(
         functools.partial(back_kernel, n_stages),
         name="backward",
         out_shape=(wide, wide, jax.ShapeDtypeStruct((rows, width), BF16)),
-        in_specs=[pl.BlockSpec(memory_space=pltpu.VMEM), ANY, ANY, ANY],
+        in_specs=[ANY] * 4,
         out_specs=(ANY, ANY, ANY),
         scratch_shapes=[
             pltpu.VMEM((width, hidden), BF16),
             pltpu.VMEM((hidden, width), BF16),
+            pltpu.VMEM((rows, width), BF16),
             pltpu.VMEM((rows, width), BF16),
             pltpu.VMEM((2, BACK_ROWS, hidden), BF16),
             pltpu.VMEM((2, BACK_ROWS, hidden), BF16),
@@ -236,10 +253,11 @@
             pltpu.VMEM((BACK_ROWS, width), F32),
             pltpu.VMEM((2, BACK_ROWS, BACK_TILE), F32),
             pltpu.VMEM((2, BACK_ROWS, BACK_TILE), F32),
-            pltpu.VMEM((STAGING, u_rows, hidden), F32),
-            pltpu.VMEM((STAGING, v_rows, width), F32),
+            pltpu.VMEM((STAGING, width, BACK_TILE), F32),
+            pltpu.VMEM((STAGING, BACK_TILE, width), F32),
             pltpu.SemaphoreType.DMA((STAGING,)),
             pltpu.SemaphoreType.DMA((STAGING,)),
+            pltpu.SemaphoreType.DMA((n_chunks,)),
             pltpu.SemaphoreType.DMA((n_chunks,)),
             pltpu.SemaphoreType.DMA((n_chunks,)),
             pltpu.SemaphoreType.DMA((n_chunks,)),
@@ -251,53 +269,99 @@
     )(acts, loss_grad, up32, down32)
 
 
-def wgrad_kernel(owner_ref, left_ref, right_ref, grad_ref, sum_ref):
+def wgrad_kernel(owner_ref, left_ref, right_ref, grad_ref, *refs):
+    sum_refs, acc_ref = refs[:-1], refs[-1]
     lead = (0,) * (len(left_ref.shape) - 2)
-    sum_ref[...] = grad_ref[0, 0]
+    acc_ref[...] = grad_ref[0, 0]
 
     def step(k, carry):
         part = span(k, WGRAD_STEP)
-        sum_ref[...] += dot_tn(left_ref[lead + (part, slice(None))], right_ref[part, :])
+        acc_ref[...] += dot_tn(left_ref[lead + (part, slice(None))], right_ref[part, :])
         return carry
 
     lax.fori_loop(0, right_ref.shape[0] // WGRAD_STEP, step, 0)
-
-
-def wgrad_call(owner, operands, in_specs, out_spec, shape, steps):
-    rows = operands[1].shape[0]
+    for p, sum_ref in enumerate(sum_refs):
+        def put(ref=sum_ref):
+            ref[...] = acc_ref[...]
+
+        if len(sum_refs) == 1:
+            put()
+        else:
+            pl.when(pl.program_id(0) == p)(put)
+
+
+def wgrad_units(kind, first, count, owner, left, right, grad):
+    rows = right.shape[0]
+    if kind == 0:
+        half, piece = left.shape[2] // 2, right.shape[1] // PIECES
+        shape = (half, piece)
+        in_specs = [
+            pl.BlockSpec((1, rows, half), lambda i, own: (0, 0, own[0])),
+            pl.BlockSpec((rows, piece), lambda i, own: (0, first + i)),
+            pl.BlockSpec((1, 1, half, piece), lambda i, own: (0, 0, own[0], first + i)),
+        ]
+    else:
+        width, piece = right.shape[1], left.shape[1] // 2 // PIECES
+        shape = (piece, width)
+        in_specs = [
+            pl.BlockSpec((rows, piece), lambda i, own: (0, own[0] * PIECES + first + i)),
+            pl.BlockSpec((rows, width), lambda i, own: (0, 0)),
+            pl.BlockSpec((1, 1, piece, width), lambda i, own: (0, 0, own[0] * PIECES + first + i, 0)),
+        ]
     return pl.pallas_call(
         wgrad_kernel,
-        out_shape=jax.ShapeDtypeStruct(shape, F32),
-        grid_spec=pltpu.PrefetchScalarGridSpec(num_scalar_prefetch=1, grid=(steps,), in_specs=in_specs, out_specs=out_spec),
+        out_shape=(jax.ShapeDtypeStruct(shape, F32),) * count,
+        grid_spec=pltpu.PrefetchScalarGridSpec(
+            num_scalar_prefetch=1,
+            grid=(count,),
+            in_specs=in_specs,
+            out_specs=(pl.BlockSpec(shape, lambda i, own: (0, 0)),) * count,
+            scratch_shapes=[pltpu.VMEM(shape, F32)],
+        ),
         compiler_params=pltpu.CompilerParams(vmem_limit_bytes=VMEM_LIMIT),
-        cost_estimate=pl.CostEstimate(flops=2 * rows * shape[0] * shape[1], bytes_accessed=15 * 1024 * 1024, transcendentals=0),
-    )(owner, *operands)
-
-
-def wgrad_up(k, owner, acts, d_pre, grad_up):
-    _, rows, width = acts.shape
-    half, piece = width // 2, d_pre.shape[1] // PIECES
-    steps = WGRAD_GRID
-    un = piece // steps
-    in_specs = [
-        pl.BlockSpec((1, rows, half), lambda i, own: (0, 0, own[0])),
-        pl.BlockSpec((rows, un), lambda i, own: (0, k * steps + i)),
-        pl.BlockSpec((1, 1, half, un), lambda i, own: (0, 0, own[0], k * steps + i)),
-    ]
-    return wgrad_call(owner, (acts, d_pre, grad_up), in_specs, pl.BlockSpec((half, un), lambda i, own: (0, i)), (half, piece), steps)
-
-
-def wgrad_down(k, owner, hid, g_own, grad_down):
-    rows, width = g_own.shape
-    piece = hid.shape[1] // 2 // PIECES
-    steps = WGRAD_GRID
-    vm = piece // steps
-    in_specs = [
-        pl.BlockSpec((rows, vm), lambda i, own: (0, (own[0] * PIECES + k) * steps + i)),
-        pl.BlockSpec((rows, width), lambda i, own: (0, 0)),
-        pl.BlockSpec((1, 1, vm, width), lambda i, own: (0, 0, (own[0] * PIECES + k) * steps + i, 0)),
-    ]
-    return wgrad_call(owner, (hid, g_own, grad_down), in_specs, pl.BlockSpec((vm, width), lambda i, own: (i, 0)), (piece, width), steps)
+        cost_estimate=pl.CostEstimate(flops=2 * rows * shape[0] * shape[1] * count, bytes_accessed=15 * 1024 * 1024, transcendentals=0),
+    )(owner, left, right, grad)
+
+
+def combine_kernel(scale, mine_ref, theirs_ref, sq_ref, gbar_ref, sq_out):
+    n_rows, cols = mine_ref.shape
+
+    def slab(i, fold):
+        rows = span(i, SLAB)
+        mean = (mine_ref[rows, :] + theirs_ref[rows, :]) * scale
+        gbar_ref[rows, :] = mean
+        part = jnp.sum((mean * mean).reshape(SLAB // 8, 8, cols), axis=0)
+        for j in range(cols // 128):
+            fold = fold + part[:, j * 128:(j + 1) * 128]
+        return fold
+
+    fold = lax.fori_loop(0, n_rows // SLAB, slab, jnp.zeros((8, 128), F32))
+    first = pl.program_id(0) == 0
+
+    @pl.when(first)
+    def _():
+        sq_out[...] = sq_ref[...] + fold
+
+    @pl.when(jnp.logical_not(first))
+    def _():
+        sq_out[...] += fold
+
+
+def combine(scale, mine, theirs, squares):
+    rows, cols = mine.shape
+    steps = 2
+    spec = pl.BlockSpec((rows // steps, cols), lambda i: (i, 0))
+    small = pl.BlockSpec((8, 128), lambda i: (0, 0))
+    return pl.pallas_call(
+        functools.partial(combine_kernel, scale),
+        name="combine",
+        out_shape=(jax.ShapeDtypeStruct((rows, cols), F32), jax.ShapeDtypeStruct((8, 128), F32)),
+        grid=(steps,),
+        in_specs=[spec, spec, small],
+        out_specs=(spec, small),
+        compiler_params=pltpu.CompilerParams(vmem_limit_bytes=VMEM_LIMIT),
+        cost_estimate=pl.CostEstimate(flops=4 * rows * cols, bytes_accessed=12 * rows * cols, transcendentals=0),
+    )(mine, theirs, squares)
 
 
 def update_kernel(n_pieces, n_alias, owner_ref, lr_ref, clip_ref, w_ref, m_ref, v_ref, *rest):
@@ -307,16 +371,21 @@
     clip, lr = clip_ref[0:1, 0:1], lr_ref[0]
 
     def run(g_ref, b_out):
-        w = w_ref[0]
-        q = clip * g_ref[...]
-        m_new = BETA1 * m_ref[0] + (1.0 - BETA1) * q
-        v_new = BETA2 * v_ref[0] + (1.0 - BETA2) * q * q
-        m_hat = m_new * (1.0 / (1.0 - BETA1 ** ADAM_STEP))
-        v_hat = v_new * (1.0 / (1.0 - BETA2 ** ADAM_STEP))
-        w_new = w - lr * (m_hat / (jnp.sqrt(v_hat) + ADAM_EPS) + WEIGHT_DECAY * w)
-        w_out[0], m_out[0], v_out[0] = w_new, m_new, v_new
-        if b_out is not None:
-            b_out[...] = w_new.astype(BF16)
+        def slab(i, carry):
+            rows = span(i, SLAB)
+            w = w_ref[0, rows, :]
+            q = clip * g_ref[rows, :]
+            m_new = BETA1 * m_ref[0, rows, :] + (1.0 - BETA1) * q
+            v_new = BETA2 * v_ref[0, rows, :] + (1.0 - BETA2) * q * q
+            m_hat = m_new * (1.0 / (1.0 - BETA1 ** ADAM_STEP))
+            v_hat = v_new * (1.0 / (1.0 - BETA2 ** ADAM_STEP))
+            w_new = w - lr * (m_hat / (jnp.sqrt(v_hat) + ADAM_EPS) + WEIGHT_DECAY * w)
+            w_out[0, rows, :], m_out[0, rows, :], v_out[0, rows, :] = w_new, m_new, v_new
+            if b_out is not None:
+                b_out[rows, :] = w_new.astype(BF16)
+            return carry
+
+        lax.fori_loop(0, g_ref.shape[0] // SLAB, slab, 0)
 
     if n_pieces == 1:
         run(g_refs[0], b_outs[0] if b_outs else None)
@@ -328,7 +397,7 @@
 def update_units(kind, first, owner, knobs, state, grads, chain, want_bf16):
     rows, cols = grads[0].shape
     n = len(grads)
-    steps = UPDATE_GRID
+    steps = 2 if n == 1 else 1
     block = rows // steps
     if kind == 0:
         spec = pl.BlockSpec((1, block, cols), lambda p, i, own: (0, own[0] * steps + i, first + p))
@@ -359,15 +428,10 @@
     )(owner, *knobs, *state, *grads, *chain)
 
 
-def norm_kernel(n_stages, n_rep, n_parts, *refs):
-    parts, (max_ref, clip_ref, mine, slots, send_sem, recv_sem) = refs[:n_parts], refs[n_parts:]
+def norm_kernel(n_stages, n_rep, sq_ref, max_ref, clip_ref, slots, send_sem, recv_sem):
     n_dev = n_stages * n_rep
     me = lax.axis_index("data") * n_stages + lax.axis_index("stage")
-    total = parts[0][0]
-    for part in parts[1:]:
-        total = total + part[0]
-    mine[...] = jnp.full(mine.shape, total, F32)
-    slots[me] = jnp.full(mine.shape, total, F32)
+    slots[me] = sq_ref[...]
 
     def place(d):
         q = lax.rem(me + d, n_dev)
@@ -380,7 +444,7 @@
     copies = []
     for d in range(1, n_dev):
         copies.append(pltpu.make_async_remote_copy(
-            src_ref=mine, dst_ref=slots.at[me], send_sem=send_sem.at[d - 1], recv_sem=recv_sem.at[d - 1],
+            src_ref=sq_ref, dst_ref=slots.at[me], send_sem=send_sem.at[d - 1], recv_sem=recv_sem.at[d - 1],
             device_id=place(d), device_id_type=MESH_ID))
         copies[-1].start()
     for copy in copies:
@@ -388,26 +452,26 @@
     square = slots[0]
     for q in range(1, n_dev):
         square = square + slots[q]
-    clip_ref[...] = jnp.minimum(1.0, max_ref[0] / (jnp.sqrt(square) + NORM_EPS))
-
-
-def clip_factor(n_stages, n_rep, parts, max_norm):
+    total = jnp.full(clip_ref.shape, jnp.sum(square), F32)
+    clip_ref[...] = jnp.minimum(1.0, max_ref[0] / (jnp.sqrt(total) + NORM_EPS))
+
+
+def clip_factor(n_stages, n_rep, squares, max_norm):
     n_dev = n_stages * n_rep
     return pl.pallas_call(
-        functools.partial(norm_kernel, n_stages, n_rep, len(parts)),
+        functools.partial(norm_kernel, n_stages, n_rep),
         name="clip_factor",
         out_shape=jax.ShapeDtypeStruct((8, 128), F32),
-        in_specs=[pl.BlockSpec(memory_space=pltpu.SMEM)] * (len(parts) + 1),
+        in_specs=[pl.BlockSpec(memory_space=pltpu.VMEM), pl.BlockSpec(memory_space=pltpu.SMEM)],
         out_specs=pl.BlockSpec(memory_space=pltpu.VMEM),
         scratch_shapes=[
-            pltpu.VMEM((8, 128), F32),
             pltpu.VMEM((n_dev, 8, 128), F32),
             pltpu.SemaphoreType.DMA((n_dev - 1,)),
             pltpu.SemaphoreType.DMA((n_dev - 1,)),
         ],
         compiler_params=pltpu.CompilerParams(collective_id=2, has_side_effects=True),
         cost_estimate=pl.CostEstimate(flops=40000000, bytes_accessed=4096, transcendentals=0),
-    )(*parts, max_norm)
+    )(squares, max_norm)
 
 
 def fwd_kernel(n_stages, n_rep, batch_ref, *refs):
@@ -544,6 +608,10 @@
     )(y)
 
 
+def part_of(parts):
+    return next(iter(parts.values()))
+
+
 def solution(mesh):
     n_stages = mesh.shape["stage"]
     n_rep = mesh.shape["data"]
@@ -558,22 +626,26 @@
         other = 1 - mine
         hid, d_pre, g_own = backward(n_stages, stage_acts, loss_grad, master_up, master_down)
 
-        units = [(kind, k) for k in range(PIECES) for kind in (0, 1)]
-
-        def wgrad(unit, owner):
-            if unit[0] == 0:
-                return wgrad_up(unit[1], owner, stage_acts, d_pre, grad_up)
-            return wgrad_down(unit[1], owner, hid, g_own, grad_down)
+        units = [(kind, first + i) for kind, first, count in GROUPS for i in range(count)]
+
+        def wgrad(group, owner):
+            kind, first, count = group
+            operands = (stage_acts, d_pre, grad_up) if kind == 0 else (hid, g_own, grad_down)
+            parts = wgrad_units(kind, first, count, owner, *operands)
+            return {(kind, first + i): parts[i] for i in range(count)}
 
         arrived, whose = {}, other
+        for group in GROUPS:
+            parts = wgrad(group, whose)
+            for unit, part in parts.items():
+                arrived[unit] = exchange(part)
+            whose = lax.optimization_barrier((other, part_of(parts)))[0]
+        gbar, squares = {}, jnp.zeros((8, 128), F32)
+        own_part = {}
+        for kind in (0, 1):
+            own_part.update(wgrad((kind, 0, PIECES), mine))
         for unit in units:
-            part = wgrad(unit, whose)
-            arrived[unit] = exchange(part)
-            whose = lax.optimization_barrier((other, part))[0]
-        gbar, squares = {}, []
-        for unit in units:
-            gbar[unit] = (wgrad(unit, mine) + arrived[unit]) * (1.0 / n_rep)
-            squares.append(jnp.reshape(jnp.sum(gbar[unit] * gbar[unit]), (1,)))
+            gbar[unit], squares = combine(1.0 / n_rep, own_part[unit], arrived[unit], squares)
         clip = clip_factor(n_stages, n_rep, squares, jnp.reshape(max_norm, (1,)))
         knobs = (jnp.reshape(learn_rate, (1,)), clip)
         gbar_other = {}

time: 845 us -> 758 us (0.90)
  Pallas kernels: 563 us -> 468 us
  waiting for transfers between devices: 220 us -> 253 us
  other arithmetic: 26 us -> 0 us
    pallas_call x25 -> x22, Pallas kernels: 216 us -> 150 us  [the longest x9 90.5 us: wgrad_units(): pl.pallas_call(wgrad_kernel, out_shape=(jax.ShapeDtypeStruct(shape, F32),...]
    ppermute x35, waiting for transfers between devices: 220 us -> 253 us  [exchange(): return lax.ppermute(x, 'data', swap)]
    reduce_sum x12 -> x0, other arithmetic: 26 us -> none  [local_step(): squares.append(jnp.reshape(jnp.sum(gbar[unit] * gbar[unit]), (1,)))]
    pallas_call x17, Pallas kernels: 102 us -> 80 us  [update_units(): pl.pallas_call(functools.partial(update_kernel, n, len(chain)), out_shape...]
  transfers between devices with their start and end apart: 35 -> 35, of which waited for: 17 -> 15; matrix products, arithmetic and copies ran while one was open for 3% -> 0% of each run, Pallas kernels for 50% -> 42%
where the time goes in v1:
time: 758 us; the launch traced here: 757 us
  Pallas kernels  468 us (62%)
  waiting for transfers between devices  253 us (33%)
  starting transfers between devices  31.2 us (4%)
    ppermute x35, waiting for transfers between devices, exchange(): return lax.ppermute(x, 'data', swap)  253 us
    pallas_call x1, Pallas kernels, forward(): pl.pallas_call(functools.partial(fwd_kernel, n_stages, n_rep), name='forw...  158 us
    pallas_call x9, Pallas kernels, wgrad_units(): pl.pallas_call(wgrad_kernel, out_shape=(jax.ShapeDtypeStruct(shape, F32),...  90.5 us
    pallas_call x17, Pallas kernels, update_units(): pl.pallas_call(functools.partial(update_kernel, n, len(chain)), out_shape...  80 us
    pallas_call x1, Pallas kernels, backward(): pl.pallas_call(functools.partial(back_kernel, n_stages), name='backward',...  74.4 us
    pallas_call x1, Pallas kernels, clip_factor(): pl.pallas_call(functools.partial(norm_kernel, n_stages, n_rep), name='cli...  33.1 us
    ppermute x35, starting transfers between devices, exchange(): return lax.ppermute(x, 'data', swap)  31.2 us
    pallas_call x12, Pallas kernels, combine(): pl.pallas_call(functools.partial(combine_kernel, scale), name='combine',...  26.8 us
  transfers between devices with their start and end apart: 35, of which 15 were waited for; matrix products, arithmetic and copies ran while one was open for 0% of the time, Pallas kernels for 42%

profile of v1, /device:TPU:3, one launch (start us, length us, event | category | flops | bytes accessed | tf_op | source)
XLA Modules:
  0.0 757.1 jit_solution(6510534878009819227)
XLA Ops:
  0.6 74.4 %backward.1 = (bf16[4096,3072]{1,0:T(8,128)(2,1)}, bf16[4096,3072]{1,0:T(8,128)(2,1)}, bf16[4096,768]{1,0:T(8,128)(2,1)}) custom-call(bf16[1,4096,768]{2,1,0:T(8,128)(2,1)} %left_ref.9, bf16[4096,768]{1,0:T(8,128)(2,1)} %dy_ref.1, f32[1,768,3072]{2,1,0:T(8,128)} %w_ref.25, f32[1,3072,768]{2,1,0:T(8,128)} %w_ref.33), custom_call_target="tpu_custom_call" | custom-call | flops 57982058496 | bytes 75497472 | tf_op jit(solution)/shard_map/backward/pallas_call | solution.py:239
  81.2 8.6 %shard_map.182 = (f32[256,768]{1,0:T(8,128)}, f32[256,768]{1,0:T(8,128)}) custom-call(s32[1]{0:T(128)S(6)} %sub.3.owner_ref, bf16[4096,3072]{1,0:T(8,128)(2,1)} %get-tuple-element.141.left_ref, bf16[4096,768]{1,0:T(8,128)(2,1)} %get-tuple-element.142.right_ref, f32[1,1,3072,768]{3,2,1,0:T(8,128)} %grad_ref.17), custom_call_target="tpu_custom_call" | custom-call | flops 3221225472 | bytes 15728640 | tf_op jit(solution)/shard_map/pallas_call | solution.py:311
  89.8 8.4 %shard_map.183 = (f32[384,512]{1,0:T(8,128)}, f32[384,512]{1,0:T(8,128)}) custom-call(s32[1]{0:T(128)S(6)} %sub.3.owner_ref, bf16[1,4096,768]{2,1,0:T(8,128)(2,1)} %left_ref.9, bf16[4096,3072]{1,0:T(8,128)(2,1)} %get-tuple-element.138.right_ref, f32[1,1,768,3072]{3,2,1,0:T(8,128)} %grad_ref.16), custom_call_target="tpu_custom_call" | custom-call | flops 3221225472 | bytes 15728640 | tf_op jit(solution)/shard_map/pallas_call | solution.py:311
  98.2 8.6 %shard_map.184 = (f32[256,768]{1,0:T(8,128)}, f32[256,768]{1,0:T(8,128)}) custom-call(s32[1]{0:T(128)S(6)} %sub.3.owner_ref, bf16[4096,3072]{1,0:T(8,128)(2,1)} %get-tuple-element.141.left_ref, bf16[4096,768]{1,0:T(8,128)(2,1)} %get-tuple-element.142.right_ref, f32[1,1,3072,768]{3,2,1,0:T(8,128)} %grad_ref.17), custom_call_target="tpu_custom_call" | custom-call | flops 3221225472 | bytes 15728640 | tf_op jit(solution)/shard_map/pallas_call | solution.py:311
  111.6 8.4 %shard_map.185 = (f32[384,512]{1,0:T(8,128)}, f32[384,512]{1,0:T(8,128)}) custom-call(s32[1]{0:T(128)S(6)} %sub.3.owner_ref, bf16[1,4096,768]{2,1,0:T(8,128)(2,1)} %left_ref.9, bf16[4096,3072]{1,0:T(8,128)(2,1)} %get-tuple-element.138.right_ref, f32[1,1,768,3072]{3,2,1,0:T(8,128)} %grad_ref.16), custom_call_target="tpu_custom_call" | custom-call | flops 3221225472 | bytes 15728640 | tf_op jit(solution)/shard_map/pallas_call | solution.py:311
  119.9 8.7 %shard_map.186 = (f32[256,768]{1,0:T(8,128)}, f32[256,768]{1,0:T(8,128)}) custom-call(s32[1]{0:T(128)S(6)} %sub.3.owner_ref, bf16[4096,3072]{1,0:T(8,128)(2,1)} %get-tuple-element.141.left_ref, bf16[4096,768]{1,0:T(8,128)(2,1)} %get-tuple-element.142.right_ref, f32[1,1,3072,768]{3,2,1,0:T(8,128)} %grad_ref.17), custom_call_target="tpu_custom_call" | custom-call | flops 3221225472 | bytes 15728640 | tf_op jit(solution)/shard_map/pallas_call | solution.py:311
  136.8 18.2 %shard_map.180 = (f32[384,512]{1,0:T(8,128)}, f32[384,512]{1,0:T(8,128)}, f32[384,512]{1,0:T(8,128)}, f32[384,512]{1,0:T(8,128)}, f32[384,512]{1,0:T(8,128)}, /*index=5*/f32[384,512]{1,0:T(8,128)}) custom-call(s32[1]{0:T(128)} %bitcast.owner_ref, bf16[1,4096,768]{2,1,0:T(8,128)(2,1)} %left_ref.9, bf16[4096,3072]{1,0:T(8,128)(2,1)} %get-tuple-element.138.right_ref, ...), custom_call_target="tpu_custom_call" | custom-call | flops 9663676416 | bytes 15728640 | tf_op jit(solution)/shard_map/pallas_call | solution.py:311
  154.9 45.3 %collective-permute-done.7.theirs_ref = f32[384,512]{1,0:T(8,128)} collective-permute-done((f32[384,512]{1,0:T(8,128)}, f32[384,512]{1,0:T(8,128)}, u32[]{:S(2)}, u32[]{:S(2)}) %collective-permute-start.7) | collective-permute-done | bytes 786464 | tf_op jit(solution)/shard_map/ppermute | solution.py:621
  201.7 15.4 %collective-permute-done.9.theirs_ref = f32[256,768]{1,0:T(8,128)} collective-permute-done((f32[256,768]{1,0:T(8,128)}, f32[256,768]{1,0:T(8,128)}, u32[]{:S(2)}, u32[]{:S(2)}) %collective-permute-start.9) | collective-permute-done | bytes 786464 | tf_op jit(solution)/shard_map/ppermute | solution.py:621
  219.7 17.5 %shard_map.188 = (f32[256,768]{1,0:T(8,128)}, f32[256,768]{1,0:T(8,128)}, f32[256,768]{1,0:T(8,128)}, f32[256,768]{1,0:T(8,128)}, f32[256,768]{1,0:T(8,128)}, /*index=5*/f32[256,768]{1,0:T(8,128)}) custom-call(s32[1]{0:T(128)} %bitcast.owner_ref, bf16[4096,3072]{1,0:T(8,128)(2,1)} %get-tuple-element.141.left_ref, ...), custom_call_target="tpu_custom_call" | custom-call | flops 9663676416 | bytes 15728640 | tf_op jit(solution)/shard_map/pallas_call | solution.py:311
  255.8 45.5 %collective-permute-done.3.theirs_ref = f32[384,512]{1,0:T(8,128)} collective-permute-done((f32[384,512]{1,0:T(8,128)}, f32[384,512]{1,0:T(8,128)}, u32[]{:S(2)}, u32[]{:S(2)}) %collective-permute-start.3) | collective-permute-done | bytes 786464 | tf_op jit(solution)/shard_map/ppermute | solution.py:621
  312.0 33.1 %clip_factor.1.clip_ref = f32[8,128]{1,0:T(8,128)} custom-call(f32[8,128]{1,0:T(8,128)} %get-tuple-element.180.sq_ref, f32[1]{0:T(128)} %bitcast.20.max_ref), custom_call_target="tpu_custom_call" | custom-call | flops 40000000 | bytes 4096 | tf_op jit(solution)/shard_map/clip_factor/pallas_call | solution.py:461
  385.8 7.3 collective-permute-done.28.refs_17_
  411.2 7.3 collective-permute-done.31.refs_20_
  419.6 40.9 %collective-permute-done.32.refs_21_ = bf16[256,768]{1,0:T(8,128)(2,1)S(1)} collective-permute-done((bf16[256,768]{1,0:T(8,128)(2,1)}, bf16[256,768]{1,0:T(8,128)(2,1)S(1)}, u32[]{:S(2)}, u32[]{:S(2)}) %collective-permute-start.32) | collective-permute-done | bytes 393248 | tf_op jit(solution)/shard_map/ppermute | solution.py:621
  461.7 7.3 collective-permute-done.33.refs_22_
  470.1 7.3 collective-permute-done.34.refs_23_
  495.5 15.7 %collective-permute-done.14.rest_1_ = f32[384,512]{1,0:T(8,128)} collective-permute-done((f32[384,512]{1,0:T(8,128)S(1)}, f32[384,512]{1,0:T(8,128)}, u32[]{:S(2)}, u32[]{:S(2)}) %collective-permute-start.14) | collective-permute-done | bytes 786464 | tf_op jit(solution)/shard_map/ppermute | solution.py:621
  512.3 15.7 %collective-permute-done.15.rest_2_ = f32[384,512]{1,0:T(8,128)} collective-permute-done((f32[384,512]{1,0:T(8,128)S(1)}, f32[384,512]{1,0:T(8,128)}, u32[]{:S(2)}, u32[]{:S(2)}) %collective-permute-start.15) | collective-permute-done | bytes 786464 | tf_op jit(solution)/shard_map/ppermute | solution.py:621
  529.2 15.6 %collective-permute-done.16.rest_3_ = f32[384,512]{1,0:T(8,128)S(1)} collective-permute-done((f32[384,512]{1,0:T(8,128)S(1)}, f32[384,512]{1,0:T(8,128)S(1)}, u32[]{:S(2)}, u32[]{:S(2)}) %collective-permute-start.16) | collective-permute-done | bytes 786464 | tf_op jit(solution)/shard_map/ppermute | solution.py:621
  545.9 15.7 %collective-permute-done.20.rest_0_ = f32[256,768]{1,0:T(8,128)S(1)} collective-permute-done((f32[256,768]{1,0:T(8,128)}, f32[256,768]{1,0:T(8,128)S(1)}, u32[]{:S(2)}, u32[]{:S(2)}) %collective-permute-start.20) | collective-permute-done | bytes 786464 | tf_op jit(solution)/shard_map/ppermute | solution.py:621
  562.8 158.3 %forward.1.y_ref = bf16[1,2,4096,768]{3,2,1,0:T(8,128)(2,1)S(1)} custom-call(bf16[2,4096,768]{2,1,0:T(8,128)(2,1)} %batch_ref.1, bf16[384,512]{1,0:T(8,128)(2,1)} %get-tuple-element.257.refs_0_, bf16[384,512]{1,0:T(8,128)(2,1)} %get-tuple-element.258.refs_1_, bf16[384,512]{1,0:T(8,128)(2,1)} %get-tuple-element.259.refs_2_, ...), custom_call_target="tpu_custom_call" | custom-call | flops 77309411328 | bytes 75497472 | tf_op jit(solution)/shard_map/forward/pallas_call | solution.py:568
  725.9 10.9 %shard_map.196 = (f32[1,768,3072]{2,1,0:T(8,128)}, f32[1,768,3072]{2,1,0:T(8,128)}, f32[1,768,3072]{2,1,0:T(8,128)}) custom-call(s32[1]{0:T(128)S(6)} %sub.3.owner_ref, f32[1]{0:T(128)} %bitcast.10.lr_ref, f32[8,128]{1,0:T(8,128)} %clip_factor.1.clip_ref, f32[1,768,3072]{2,1,0:T(8,128)} %w_ref.25, ...), custom_call_target="tpu_custom_call", output_to_operand_aliasing={{0}: (10, {}), {1}: (11, {}), {2}: (12, {})} | custom-call | flops 23592960 | bytes 22020096 | tf_op jit(solution)/shard_map/pallas_call | solution.py:416
  740.5 10.8 %shard_map.204 = (f32[1,3072,768]{2,1,0:T(8,128)}, f32[1,3072,768]{2,1,0:T(8,128)}, f32[1,3072,768]{2,1,0:T(8,128)}) custom-call(s32[1]{0:T(128)S(6)} %sub.3.owner_ref, f32[1]{0:T(128)} %bitcast.18.lr_ref, f32[8,128]{1,0:T(8,128)} %clip_factor.1.clip_ref, f32[1,3072,768]{2,1,0:T(8,128)} %w_ref.33, ...), custom_call_target="tpu_custom_call", output_to_operand_aliasing={{0}: (10, {}), {1}: (11, {}), {2}: (12, {})} | custom-call | flops 23592960 | bytes 22020096 | tf_op jit(solution)/shard_map/pallas_call | solution.py:416
  (131 shorter events, 150.2 us)
Async XLA Ops:
  108.3 93.1 %collective-permute-start.8 = (f32[384,512]{1,0:T(8,128)}, f32[384,512]{1,0:T(8,128)S(1)}, u32[]{:S(2)}, u32[]{:S(2)}) collective-permute-start(f32[384,512]{1,0:T(8,128)} %get-tuple-element.145), channel_id=1, source_target_pairs={{0,4},{4,0},{1,5},{5,1},{2,6},{6,2},{3,7},{7,3}} | collective-permute-start | bytes 2359304 | tf_op jit(solution)/shard_map/ppermute | solution.py:621
  109.4 108.8 %collective-permute-start.10 = (f32[256,768]{1,0:T(8,128)}, f32[256,768]{1,0:T(8,128)S(1)}, u32[]{:S(2)}, u32[]{:S(2)}) collective-permute-start(f32[256,768]{1,0:T(8,128)} %get-tuple-element.143), channel_id=1, source_target_pairs={{0,4},{4,0},{1,5},{5,1},{2,6},{6,2},{3,7},{7,3}} | collective-permute-start | bytes 2359304 | tf_op jit(solution)/shard_map/ppermute | solution.py:621
  109.7 108.8 %collective-permute-start.11 = (f32[384,512]{1,0:T(8,128)}, f32[384,512]{1,0:T(8,128)}, u32[]{:S(2)}, u32[]{:S(2)}) collective-permute-start(f32[384,512]{1,0:T(8,128)} %shard_map.181), channel_id=1, source_target_pairs={{0,4},{4,0},{1,5},{5,1},{2,6},{6,2},{3,7},{7,3}} | collective-permute-start | bytes 2359304 | tf_op jit(solution)/shard_map/ppermute | solution.py:621
  135.3 65.0 %collective-permute-start.7 = (f32[384,512]{1,0:T(8,128)}, f32[384,512]{1,0:T(8,128)}, u32[]{:S(2)}, u32[]{:S(2)}) collective-permute-start(f32[384,512]{1,0:T(8,128)} %get-tuple-element.163), channel_id=1, source_target_pairs={{0,4},{4,0},{1,5},{5,1},{2,6},{6,2},{3,7},{7,3}} | collective-permute-start | bytes 2359304 | tf_op jit(solution)/shard_map/ppermute | solution.py:621
  135.8 81.4 %collective-permute-start.9 = (f32[256,768]{1,0:T(8,128)}, f32[256,768]{1,0:T(8,128)}, u32[]{:S(2)}, u32[]{:S(2)}) collective-permute-start(f32[256,768]{1,0:T(8,128)} %get-tuple-element.166), channel_id=1, source_target_pairs={{0,4},{4,0},{1,5},{5,1},{2,6},{6,2},{3,7},{7,3}} | collective-permute-start | bytes 2359304 | tf_op jit(solution)/shard_map/ppermute | solution.py:621
  200.3 103.3 %collective-permute-start.2 = (f32[256,768]{1,0:T(8,128)}, f32[256,768]{1,0:T(8,128)S(1)}, u32[]{:S(2)}, u32[]{:S(2)}) collective-permute-start(f32[256,768]{1,0:T(8,128)} %get-tuple-element.151), channel_id=1, source_target_pairs={{0,4},{4,0},{1,5},{5,1},{2,6},{6,2},{3,7},{7,3}} | collective-permute-start | bytes 2359304 | tf_op jit(solution)/shard_map/ppermute | solution.py:621
  201.4 52.1 %collective-permute-start.4 = (f32[384,512]{1,0:T(8,128)}, f32[384,512]{1,0:T(8,128)}, u32[]{:S(2)}, u32[]{:S(2)}) collective-permute-start(f32[384,512]{1,0:T(8,128)} %get-tuple-element.149), channel_id=1, source_target_pairs={{0,4},{4,0},{1,5},{5,1},{2,6},{6,2},{3,7},{7,3}} | collective-permute-start | bytes 2359304 | tf_op jit(solution)/shard_map/ppermute | solution.py:621
  217.1 91.8 %collective-permute-start = (f32[384,512]{1,0:T(8,128)}, f32[384,512]{1,0:T(8,128)S(1)}, u32[]{:S(2)}, u32[]{:S(2)}) collective-permute-start(f32[384,512]{1,0:T(8,128)} %shard_map.187), channel_id=1, source_target_pairs={{0,4},{4,0},{1,5},{5,1},{2,6},{6,2},{3,7},{7,3}} | collective-permute-start | bytes 2359304 | tf_op jit(solution)/shard_map/ppermute | solution.py:621
  218.3 88.4 %collective-permute-start.1 = (f32[256,768]{1,0:T(8,128)}, f32[256,768]{1,0:T(8,128)}, u32[]{:S(2)}, u32[]{:S(2)}) collective-permute-start(f32[256,768]{1,0:T(8,128)} %get-tuple-element.154), channel_id=1, source_target_pairs={{0,4},{4,0},{1,5},{5,1},{2,6},{6,2},{3,7},{7,3}} | collective-permute-start | bytes 2359304 | tf_op jit(solution)/shard_map/ppermute | solution.py:621
  218.6 82.8 %collective-permute-start.3 = (f32[384,512]{1,0:T(8,128)}, f32[384,512]{1,0:T(8,128)}, u32[]{:S(2)}, u32[]{:S(2)}) collective-permute-start(f32[384,512]{1,0:T(8,128)} %get-tuple-element.157), channel_id=1, source_target_pairs={{0,4},{4,0},{1,5},{5,1},{2,6},{6,2},{3,7},{7,3}} | collective-permute-start | bytes 2359304 | tf_op jit(solution)/shard_map/ppermute | solution.py:621
  384.7 93.8 %collective-permute-start.12 = (f32[384,512]{1,0:T(8,128)S(1)}, f32[384,512]{1,0:T(8,128)}, u32[]{:S(2)}, u32[]{:S(2)}) collective-permute-start(f32[384,512]{1,0:T(8,128)S(1)} %copy-done.4), channel_id=1, source_target_pairs={{0,4},{4,0},{1,5},{5,1},{2,6},{6,2},{3,7},{7,3}} | collective-permute-start | bytes 2359304 | tf_op jit(solution)/shard_map/ppermute | solution.py:621
  393.1 85.7 %collective-permute-start.17 = (f32[384,512]{1,0:T(8,128)S(1)}, f32[384,512]{1,0:T(8,128)}, u32[]{:S(2)}, u32[]{:S(2)}) collective-permute-start(f32[384,512]{1,0:T(8,128)S(1)} %copy-done), channel_id=1, source_target_pairs={{0,4},{4,0},{1,5},{5,1},{2,6},{6,2},{3,7},{7,3}} | collective-permute-start | bytes 2359304 | tf_op jit(solution)/shard_map/ppermute | solution.py:621
  405.6 54.9 %collective-permute-start.32 = (bf16[256,768]{1,0:T(8,128)(2,1)}, bf16[256,768]{1,0:T(8,128)(2,1)S(1)}, u32[]{:S(2)}, u32[]{:S(2)}) collective-permute-start(bf16[256,768]{1,0:T(8,128)(2,1)} %get-tuple-element.265.refs_9_), channel_id=1, source_target_pairs={{0,4},{4,0},{1,5},{5,1},{2,6},{6,2},{3,7},{7,3}} | collective-permute-start | bytes 1179656 | tf_op jit(solution)/shard_map/ppermute | solution.py:621
  410.1 58.9 %collective-permute-start.33 = (bf16[256,768]{1,0:T(8,128)(2,1)}, bf16[256,768]{1,0:T(8,128)(2,1)S(1)}, u32[]{:S(2)}, u32[]{:S(2)}) collective-permute-start(bf16[256,768]{1,0:T(8,128)(2,1)} %get-tuple-element.266.refs_10_), channel_id=1, source_target_pairs={{0,4},{4,0},{1,5},{5,1},{2,6},{6,2},{3,7},{7,3}} | collective-permute-start | bytes 1179656 | tf_op jit(solution)/shard_map/ppermute | solution.py:621
  418.5 58.9 %collective-permute-start.34 = (bf16[256,768]{1,0:T(8,128)(2,1)}, bf16[256,768]{1,0:T(8,128)(2,1)S(1)}, u32[]{:S(2)}, u32[]{:S(2)}) collective-permute-start(bf16[256,768]{1,0:T(8,128)(2,1)} %get-tuple-element.267.refs_11_), channel_id=1, source_target_pairs={{0,4},{4,0},{1,5},{5,1},{2,6},{6,2},{3,7},{7,3}} | collective-permute-start | bytes 1179656 | tf_op jit(solution)/shard_map/ppermute | solution.py:621
  468.9 42.2 %collective-permute-start.14 = (f32[384,512]{1,0:T(8,128)S(1)}, f32[384,512]{1,0:T(8,128)}, u32[]{:S(2)}, u32[]{:S(2)}) collective-permute-start(f32[384,512]{1,0:T(8,128)S(1)} %copy-done.1), channel_id=1, source_target_pairs={{0,4},{4,0},{1,5},{5,1},{2,6},{6,2},{3,7},{7,3}} | collective-permute-start | bytes 2359304 | tf_op jit(solution)/shard_map/ppermute | solution.py:621
  477.4 50.7 %collective-permute-start.15 = (f32[384,512]{1,0:T(8,128)S(1)}, f32[384,512]{1,0:T(8,128)}, u32[]{:S(2)}, u32[]{:S(2)}) collective-permute-start(f32[384,512]{1,0:T(8,128)S(1)} %copy-done.2), channel_id=1, source_target_pairs={{0,4},{4,0},{1,5},{5,1},{2,6},{6,2},{3,7},{7,3}} | collective-permute-start | bytes 2359304 | tf_op jit(solution)/shard_map/ppermute | solution.py:621
  478.5 66.2 %collective-permute-start.16 = (f32[384,512]{1,0:T(8,128)S(1)}, f32[384,512]{1,0:T(8,128)S(1)}, u32[]{:S(2)}, u32[]{:S(2)}) collective-permute-start(f32[384,512]{1,0:T(8,128)S(1)} %copy-done.3), channel_id=1, source_target_pairs={{0,4},{4,0},{1,5},{5,1},{2,6},{6,2},{3,7},{7,3}} | collective-permute-start | bytes 2359304 | tf_op jit(solution)/shard_map/ppermute | solution.py:621
  478.8 82.8 %collective-permute-start.20 = (f32[256,768]{1,0:T(8,128)}, f32[256,768]{1,0:T(8,128)S(1)}, u32[]{:S(2)}, u32[]{:S(2)}) collective-permute-start(f32[256,768]{1,0:T(8,128)} %get-tuple-element.224.rest_0_), channel_id=1, source_target_pairs={{0,4},{4,0},{1,5},{5,1},{2,6},{6,2},{3,7},{7,3}} | collective-permute-start | bytes 2359304 | tf_op jit(solution)/shard_map/ppermute | solution.py:621
  494.3 256.9 %collective-permute-start.18 = (f32[256,768]{1,0:T(8,128)}, f32[256,768]{1,0:T(8,128)}, u32[]{:S(2)}, u32[]{:S(2)}) collective-permute-start(f32[256,768]{1,0:T(8,128)} %get-tuple-element.220.rest_0_), channel_id=1, source_target_pairs={{0,4},{4,0},{1,5},{5,1},{2,6},{6,2},{3,7},{7,3}} | collective-permute-start | bytes 2359304 | tf_op jit(solution)/shard_map/ppermute | solution.py:621
  511.2 240.1 %collective-permute-start.19 = (f32[256,768]{1,0:T(8,128)}, f32[256,768]{1,0:T(8,128)}, u32[]{:S(2)}, u32[]{:S(2)}) collective-permute-start(f32[256,768]{1,0:T(8,128)} %get-tuple-element.222.rest_0_), channel_id=1, source_target_pairs={{0,4},{4,0},{1,5},{5,1},{2,6},{6,2},{3,7},{7,3}} | collective-permute-start | bytes 2359304 | tf_op jit(solution)/shard_map/ppermute | solution.py:621
  528.0 212.4 %collective-permute-start.21 = (f32[256,768]{1,0:T(8,128)}, f32[256,768]{1,0:T(8,128)}, u32[]{:S(2)}, u32[]{:S(2)}) collective-permute-start(f32[256,768]{1,0:T(8,128)} %get-tuple-element.226.rest_0_), channel_id=1, source_target_pairs={{0,4},{4,0},{1,5},{5,1},{2,6},{6,2},{3,7},{7,3}} | collective-permute-start | bytes 2359304 | tf_op jit(solution)/shard_map/ppermute | solution.py:621
  544.8 195.7 %collective-permute-start.22 = (f32[256,768]{1,0:T(8,128)}, f32[256,768]{1,0:T(8,128)}, u32[]{:S(2)}, u32[]{:S(2)}) collective-permute-start(f32[256,768]{1,0:T(8,128)} %get-tuple-element.228.rest_0_), channel_id=1, source_target_pairs={{0,4},{4,0},{1,5},{5,1},{2,6},{6,2},{3,7},{7,3}} | collective-permute-start | bytes 2359304 | tf_op jit(solution)/shard_map/ppermute | solution.py:621
  561.6 178.8 %collective-permute-start.23 = (f32[256,768]{1,0:T(8,128)}, f32[256,768]{1,0:T(8,128)}, u32[]{:S(2)}, u32[]{:S(2)}) collective-permute-start(f32[256,768]{1,0:T(8,128)} %get-tuple-element.230.rest_0_), channel_id=1, source_target_pairs={{0,4},{4,0},{1,5},{5,1},{2,6},{6,2},{3,7},{7,3}} | collective-permute-start | bytes 2359304 | tf_op jit(solution)/shard_map/ppermute | solution.py:621
  (32 other events, 777.4 us)

commit v2 on v1

--- a/solution.py
+++ b/solution.py
@@ -19,6 +19,7 @@
 
 BACK_ROWS = 256
 FWD_ROWS = 256
+HEAD = 128
 BACK_TILE = 512
 FWD_TILE = 512
 PIECES = 6
@@ -26,8 +27,8 @@
 GROUPS = ((0, 0, 1), (1, 0, 2), (0, 1, 2), (1, 2, 2), (0, 3, 2), (1, 4, 2), (0, 5, 1))
 TAIL = ((1, 0, 4), (0, 1, 5), (1, 4, 6), (0, 5, 6))
 STAGING = 3
-WGRAD_STEP = 4096
-SLAB = 32
+WGRAD_STEP = 2048
+SLAB = 16
 
 BF16 = jnp.bfloat16
 F32 = jnp.float32
@@ -52,7 +53,15 @@
 
 
 def span(index, size):
+    if isinstance(index, int):
+        return pl.ds(index * size, size)
     return pl.ds(pl.multiple_of(index * size, size), size)
+
+
+def chunk_rows(c, total, size):
+    if isinstance(c, int):
+        return pl.ds(0 if c == 0 else total - HEAD, HEAD)
+    return pl.ds(pl.multiple_of(HEAD + (c - 1) * size, HEAD), size)
 
 
 def tanh_part(x, sq):
@@ -93,7 +102,8 @@
     last = n_stages - 1
     rows_all = g_buf.shape[0]
     hidden = up_ref.shape[1]
-    n_chunks = rows_all // BACK_ROWS
+    n_chunks = (rows_all - 2 * HEAD) // BACK_ROWS + 2
+    final = n_chunks - 1
     n_tiles = hidden // BACK_TILE
 
     def tile_copies(j):
@@ -102,7 +112,7 @@
                 pltpu.make_async_copy(down32_ref.at[0, cols, :], stage_v.at[slot], v_sem.at[slot]))
 
     def rows_of(c):
-        return pl.ds(c * BACK_ROWS, BACK_ROWS) if isinstance(c, int) else span(c, BACK_ROWS)
+        return chunk_rows(c, rows_all, BACK_ROWS)
 
     def a_copy(c):
         return pltpu.make_async_copy(acts_ref.at[0, rows_of(c), :], a_buf.at[rows_of(c), :], a_sem.at[c])
@@ -110,23 +120,20 @@
     def dy_copy(c):
         return pltpu.make_async_copy(dy_ref.at[rows_of(c), :], g_buf.at[rows_of(c), :], recv_sem.at[c])
 
-    a_copy(0).start()
-
-    @pl.when(stage == last)
-    def _():
-        dy_copy(0).start()
-
+    def load(c):
+        a_copy(c).start()
+
+        @pl.when(stage == last)
+        def _():
+            dy_copy(c).start()
+
+    load(0)
     for j in range(STAGING):
         for copy in tile_copies(j):
             copy.start()
 
     def load_rest(c, carry):
-        a_copy(c).start()
-
-        @pl.when(stage == last)
-        def _():
-            dy_copy(c).start()
-
+        load(c)
         return carry
 
     def cast_tile(j):
@@ -139,7 +146,8 @@
             for copy in tile_copies(j + STAGING):
                 copy.start()
         if j == n_tiles - STAGING:
-            lax.fori_loop(1, n_chunks, load_rest, 0)
+            lax.fori_loop(1, final, load_rest, 0)
+            load(final)
 
     meet_neighbours(stage, n_stages)
 
@@ -149,21 +157,28 @@
             send_sem=send_sem.at[c], recv_sem=recv_sem.at[c],
             device_id={"stage": stage - 1}, device_id_type=MESH_ID)
 
-    def out_copies(c, slot):
-        return (pltpu.make_async_copy(h_buf.at[slot], hid_ref.at[rows_of(c), :], h_sem.at[slot]),
-                pltpu.make_async_copy(p_buf.at[slot], dpre_ref.at[rows_of(c), :], p_sem.at[slot]))
+    def slot_of(c):
+        return 2 if isinstance(c, int) else lax.rem(c, 2)
+
+    def out_copies(c):
+        slot, size = slot_of(c), pl.ds(0, HEAD if isinstance(c, int) else BACK_ROWS)
+        return (pltpu.make_async_copy(h_buf.at[slot, size, :], hid_ref.at[rows_of(c), :], h_sem.at[slot]),
+                pltpu.make_async_copy(p_buf.at[slot, size, :], dpre_ref.at[rows_of(c), :], p_sem.at[slot]))
 
     def gown_copy(c):
         return pltpu.make_async_copy(g_buf.at[rows_of(c), :], gown_ref.at[rows_of(c), :], gown_sem.at[c])
 
     def chunk(c, carry, casting=False):
-        slot = c % 2 if casting else lax.rem(c, 2)
-        rows = rows_of(c)
-        if not casting:
-            @pl.when(c >= 2)
+        slot, rows = slot_of(c), rows_of(c)
+        size = pl.ds(0, HEAD if isinstance(c, int) else BACK_ROWS)
+        if not isinstance(c, int):
+            @pl.when(c >= 3)
             def _():
-                for copy in out_copies(c - 2, slot):
+                for copy in out_copies(c - 2):
                     copy.wait()
+        elif c == final:
+            for copy in out_copies(0):
+                copy.wait()
 
         a_copy(c).wait()
         dy_copy(c).wait()
@@ -173,29 +188,29 @@
             if casting:
                 cast_tile(j)
             cols = pl.ds(j * BACK_TILE, BACK_TILE)
-            pre_buf[j % 2] = dot_nn(a_buf[rows, :], up_ref[:, cols])
-            dh_buf[j % 2] = dot_nt(g_buf[rows, :], down_ref[cols, :])
+            pre_buf[j % 2, size, :] = dot_nn(a_buf[rows, :], up_ref[:, cols])
+            dh_buf[j % 2, size, :] = dot_nt(g_buf[rows, :], down_ref[cols, :])
 
         def rest(j):
             cols = pl.ds(j * BACK_TILE, BACK_TILE)
-            value, slope = gelu_pair(pre_buf[j % 2])
-            h_buf[slot, :, cols] = value.astype(BF16)
-            d_pre = (dh_buf[j % 2] * slope).astype(BF16)
-            p_buf[slot, :, cols] = d_pre
+            value, slope = gelu_pair(pre_buf[j % 2, size, :])
+            h_buf[slot, size, cols] = value.astype(BF16)
+            d_pre = (dh_buf[j % 2, size, :] * slope).astype(BF16)
+            p_buf[slot, size, cols] = d_pre
             part = dot_nt(d_pre, up_ref[:, cols])
             if j == 0:
-                acc_ref[...] = g_buf[rows, :].astype(F32) + part
+                acc_ref[size, :] = g_buf[rows, :].astype(F32) + part
             elif j < n_tiles - 1:
-                acc_ref[...] += part
+                acc_ref[size, :] += part
             else:
-                dx_buf[rows, :] = (acc_ref[...] + part).astype(BF16)
+                dx_buf[rows, :] = (acc_ref[size, :] + part).astype(BF16)
 
         products(0)
         for j in range(n_tiles):
             if j + 1 < n_tiles:
                 products(j + 1)
             rest(j)
-        for copy in out_copies(c, slot):
+        for copy in out_copies(c):
             copy.start()
 
         @pl.when(stage > 0)
@@ -212,12 +227,10 @@
     def _():
         for j in range(n_tiles):
             cast_tile(j)
-
-    lax.fori_loop(stage // last, n_chunks, chunk, 0)
-
-    for c in (n_chunks - 2, n_chunks - 1):
-        for copy in out_copies(c, c % 2):
-            copy.wait()
+        chunk(0, 0)
+
+    lax.fori_loop(1, final, chunk, 0)
+    chunk(final, 0)
 
     def finish(c, carry):
         gown_copy(c).wait()
@@ -228,13 +241,20 @@
 
         return carry
 
-    lax.fori_loop(0, n_chunks, finish, 0)
+    for c in (final - 2, final - 1):
+        for copy in out_copies(jnp.int32(c)):
+            copy.wait()
+    for copy in out_copies(final):
+        copy.wait()
+    finish(0, 0)
+    lax.fori_loop(1, final, finish, 0)
+    finish(final, 0)
 
 
 def backward(n_stages, acts, loss_grad, up32, down32):
     _, rows, width = acts.shape
     hidden = up32.shape[2]
-    n_chunks = rows // BACK_ROWS
+    n_chunks = (rows - 2 * HEAD) // BACK_ROWS + 2
     wide = jax.ShapeDtypeStruct((rows, hidden), BF16)
     return pl.pallas_call(
         functools.partial(back_kernel, n_stages),
@@ -247,8 +267,8 @@
             pltpu.VMEM((hidden, width), BF16),
             pltpu.VMEM((rows, width), BF16),
             pltpu.VMEM((rows, width), BF16),
-            pltpu.VMEM((2, BACK_ROWS, hidden), BF16),
-            pltpu.VMEM((2, BACK_ROWS, hidden), BF16),
+            pltpu.VMEM((3, BACK_ROWS, hidden), BF16),
+            pltpu.VMEM((3, BACK_ROWS, hidden), BF16),
             pltpu.VMEM((rows, width), BF16),
             pltpu.VMEM((BACK_ROWS, width), F32),
             pltpu.VMEM((2, BACK_ROWS, BACK_TILE), F32),
@@ -261,8 +281,8 @@
             pltpu.SemaphoreType.DMA((n_chunks,)),
             pltpu.SemaphoreType.DMA((n_chunks,)),
             pltpu.SemaphoreType.DMA((n_chunks,)),
-            pltpu.SemaphoreType.DMA((2,)),
-            pltpu.SemaphoreType.DMA((2,)),
+            pltpu.SemaphoreType.DMA((3,)),
+            pltpu.SemaphoreType.DMA((3,)),
         ],
         compiler_params=pltpu.CompilerParams(collective_id=0, has_side_effects=True, vmem_limit_bytes=VMEM_LIMIT),
         cost_estimate=pl.CostEstimate(flops=6 * rows * width * hidden, bytes_accessed=6 * rows * hidden, transcendentals=rows * hidden),
@@ -364,10 +384,9 @@
     )(mine, theirs, squares)
 
 
-def update_kernel(n_pieces, n_alias, owner_ref, lr_ref, clip_ref, w_ref, m_ref, v_ref, *rest):
+def update_kernel(n_pieces, n_alias, want_bf16, owner_ref, lr_ref, clip_ref, w_ref, m_ref, v_ref, *rest):
     g_refs = rest[:n_pieces]
-    w_out, m_out, v_out = rest[n_pieces + n_alias:n_pieces + n_alias + 3]
-    b_outs = rest[n_pieces + n_alias + 3:]
+    w_out, m_out, v_out, last_out = rest[n_pieces + n_alias:]
     clip, lr = clip_ref[0:1, 0:1], lr_ref[0]
 
     def run(g_ref, b_out):
@@ -388,10 +407,12 @@
         lax.fori_loop(0, g_ref.shape[0] // SLAB, slab, 0)
 
     if n_pieces == 1:
-        run(g_refs[0], b_outs[0] if b_outs else None)
+        run(g_refs[0], last_out if want_bf16 else None)
     else:
         for p in range(n_pieces):
             pl.when(pl.program_id(0) == p)(functools.partial(run, g_refs[p], None))
+    if not want_bf16:
+        last_out[...] = clip_ref[...]
 
 
 def update_units(kind, first, owner, knobs, state, grads, chain, want_bf16):
@@ -412,9 +433,12 @@
     if want_bf16:
         out_shape += (jax.ShapeDtypeStruct((rows, cols), BF16),)
         out_specs += (piece_spec(0),)
+    else:
+        out_shape += (jax.ShapeDtypeStruct((8, 128), F32),)
+        out_specs += (pl.BlockSpec((8, 128), lambda p, i, own: (0, 0)),)
     size = n * rows * cols
     return pl.pallas_call(
-        functools.partial(update_kernel, n, len(chain)),
+        functools.partial(update_kernel, n, len(chain), want_bf16),
         out_shape=out_shape,
         grid_spec=pltpu.PrefetchScalarGridSpec(
             num_scalar_prefetch=1,
@@ -481,13 +505,17 @@
     stage = lax.axis_index("stage")
     me = lax.axis_index("data")
     last = n_stages - 1
-    n_chunks = x_buf.shape[0]
+    total = x_buf.shape[0]
     hidden = up_ref.shape[1]
     n_tiles = hidden // FWD_TILE
-    chunks_per_micro = n_chunks // batch_ref.shape[0]
-
-    def batch_chunk(ref, c, lead):
-        return ref.at[lead + (c // chunks_per_micro, span(lax.rem(c, chunks_per_micro), FWD_ROWS), slice(None))]
+    n_chunks = (total - 2 * HEAD) // FWD_ROWS + 2
+    final = n_chunks - 1
+
+    def rows_of(c):
+        return chunk_rows(c, total, FWD_ROWS)
+
+    def batch_copy(c):
+        return pltpu.make_async_copy(batch_ref.at[rows_of(c), :], x_buf.at[rows_of(c), :], recv_sem.at[c])
 
     copies = []
     for side in range(n_rep):
@@ -507,10 +535,12 @@
     @pl.when(stage == 0)
     def _():
         def load(c, carry):
-            pltpu.make_async_copy(batch_chunk(batch_ref, c, ()), x_buf.at[c], recv_sem.at[c]).start()
+            batch_copy(c).start()
             return carry
 
-        lax.fori_loop(0, n_chunks, load, 0)
+        load(0, 0)
+        lax.fori_loop(1, final, load, 0)
+        load(final, 0)
 
     meet_neighbours(stage, n_stages)
     for copy in copies:
@@ -518,25 +548,27 @@
 
     def send_of(c):
         return pltpu.make_async_remote_copy(
-            src_ref=batch_chunk(out_ref, c, (0,)), dst_ref=x_buf.at[c],
+            src_ref=out_ref.at[rows_of(c), :], dst_ref=x_buf.at[rows_of(c), :],
             send_sem=send_sem.at[c], recv_sem=recv_sem.at[c],
             device_id={"stage": stage + 1}, device_id_type=MESH_ID)
 
     def chunk(c, carry):
-        pltpu.make_async_copy(batch_chunk(batch_ref, c, ()), x_buf.at[c], recv_sem.at[c]).wait()
+        rows = rows_of(c)
+        size = pl.ds(0, HEAD if isinstance(c, int) else FWD_ROWS)
+        batch_copy(c).wait()
 
         def products(j):
-            pre_buf[j % 2] = dot_nn(x_buf[c], up_ref[:, pl.ds(j * FWD_TILE, FWD_TILE)])
+            pre_buf[j % 2, size, :] = dot_nn(x_buf[rows, :], up_ref[:, pl.ds(j * FWD_TILE, FWD_TILE)])
 
         def rest(j):
-            hid = gelu_value(pre_buf[j % 2]).astype(BF16)
+            hid = gelu_value(pre_buf[j % 2, size, :]).astype(BF16)
             part = dot_nn(hid, down_ref[pl.ds(j * FWD_TILE, FWD_TILE), :])
             if j == 0:
-                acc_ref[...] = x_buf[c].astype(F32) + part
+                acc_ref[size, :] = x_buf[rows, :].astype(F32) + part
             elif j < n_tiles - 1:
-                acc_ref[...] += part
+                acc_ref[size, :] += part
             else:
-                out_ref[0, c // chunks_per_micro, span(lax.rem(c, chunks_per_micro), FWD_ROWS), :] = (acc_ref[...] + part).astype(BF16)
+                out_ref[rows, :] = (acc_ref[size, :] + part).astype(BF16)
 
         products(0)
         for j in range(n_tiles):
@@ -550,7 +582,9 @@
 
         return carry
 
-    lax.fori_loop(0, n_chunks, chunk, 0)
+    chunk(0, 0)
+    lax.fori_loop(1, final, chunk, 0)
+    chunk(final, 0)
 
     @pl.when(stage < last)
     def _():
@@ -558,23 +592,26 @@
             send_of(c).wait_send()
             return carry
 
-        lax.fori_loop(0, n_chunks, finish, 0)
+        finish(0, 0)
+        lax.fori_loop(1, final, finish, 0)
+        finish(final, 0)
 
 
 def forward(n_stages, n_rep, next_batch, weights):
     n_micro, rows, width = next_batch.shape
+    total = n_micro * rows
     hidden = PIECES * weights[0].shape[1]
-    n_chunks = n_micro * rows // FWD_ROWS
+    n_chunks = (total - 2 * HEAD) // FWD_ROWS + 2
     return pl.pallas_call(
         functools.partial(fwd_kernel, n_stages, n_rep),
         name="forward",
-        out_shape=pltpu.VMEM((1, n_micro, rows, width), BF16),
+        out_shape=pltpu.VMEM((total, width), BF16),
         in_specs=[ANY] * (1 + len(weights)),
         out_specs=pl.BlockSpec(memory_space=pltpu.VMEM),
         scratch_shapes=[
             pltpu.VMEM((width, hidden), BF16),
             pltpu.VMEM((hidden, width), BF16),
-            pltpu.VMEM((n_chunks, FWD_ROWS, width), BF16),
+            pltpu.VMEM((total, width), BF16),
             pltpu.VMEM((FWD_ROWS, width), F32),
             pltpu.VMEM((2, FWD_ROWS, FWD_TILE), F32),
             pltpu.SemaphoreType.DMA((len(weights),)),
@@ -583,14 +620,14 @@
         ],
         compiler_params=pltpu.CompilerParams(collective_id=1, has_side_effects=True, vmem_limit_bytes=FWD_VMEM),
         cost_estimate=pl.CostEstimate(flops=4 * n_micro * rows * width * hidden, bytes_accessed=6 * rows * hidden, transcendentals=n_micro * rows * hidden),
-    )(next_batch, *weights)
+    )(next_batch.reshape(total, width), *weights)
 
 
 def store_kernel(y_ref, out_ref, sem):
-    copies = []
-    for i in range(y_ref.shape[1]):
-        copies.append(pltpu.make_async_copy(y_ref.at[0, i], out_ref.at[0, i], sem.at[i]))
-        copies[-1].start()
+    half = y_ref.shape[0] // 2
+    copies = [pltpu.make_async_copy(y_ref.at[span(i, half), :], out_ref.at[span(i, half), :], sem.at[i]) for i in range(2)]
+    for copy in copies:
+        copy.start()
     for copy in copies:
         copy.wait()
 
@@ -602,7 +639,7 @@
         out_shape=jax.ShapeDtypeStruct(y.shape, y.dtype),
         in_specs=[pl.BlockSpec(memory_space=pltpu.VMEM)],
         out_specs=ANY,
-        scratch_shapes=[pltpu.SemaphoreType.DMA((y.shape[1],))],
+        scratch_shapes=[pltpu.SemaphoreType.DMA((2,))],
         compiler_params=pltpu.CompilerParams(vmem_limit_bytes=STORE_VMEM),
         cost_estimate=pl.CostEstimate(flops=4000000, bytes_accessed=2 * y.size, transcendentals=0),
     )(y)
@@ -659,9 +696,11 @@
             chain[unit[0]] = res[:3]
             return res[3]
 
-        def update_group(kind, first, stop):
+        def update_group(kind, first, stop, clip):
             grads = [gbar_other[kind, k] for k in range(first, stop)]
-            chain[kind] = update_units(kind, first, other, knobs, state[kind], grads, chain[kind], False)
+            res = update_units(kind, first, other, (knobs[0], clip), state[kind], grads, chain[kind], False)
+            chain[kind] = res[:3]
+            return res[3]
 
         late = [unit for unit in units if unit not in F32_FIRST]
         own_w, other_w = {}, {}
@@ -678,9 +717,9 @@
         for side in (own_w, other_w):
             for kind in (0, 1):
                 weights += [side[kind, k] for k in range(PIECES)]
-        stage_outs = store(forward(n_stages, n_rep, next_batch, weights))
+        stage_outs = store(forward(n_stages, n_rep, next_batch, weights)).reshape((1,) + next_batch.shape)
         for kind, first, stop in TAIL:
-            update_group(kind, first, stop)
+            clip = update_group(kind, first, stop, clip)
         (new_up, new_m1_up, new_m2_up), (new_down, new_m1_down, new_m2_down) = chain
         return (new_up, new_down, new_m1_up, new_m1_down, new_m2_up, new_m2_down, stage_outs)
 

time: 758 us -> 764 us (level)
  Pallas kernels: 468 us -> 480 us
  transfers between devices with their start and end apart: 35 -> 35, of which waited for: 15 -> 15; matrix products, arithmetic and copies ran while one was open for 0% -> 0% of each run, Pallas kernels for 42% -> 43%
where the time goes in v2:
time: 764 us; the launch traced here: 763 us
  Pallas kernels  480 us (63%)
  waiting for transfers between devices  247 us (32%)
  starting transfers between devices  31.6 us (4%)
    ppermute x35, waiting for transfers between devices, exchange(): return lax.ppermute(x, 'data', swap)  247 us
    pallas_call x1, Pallas kernels, forward(): pl.pallas_call(functools.partial(fwd_kernel, n_stages, n_rep), name='forw...  157 us
    pallas_call x9, Pallas kernels, wgrad_units(): pl.pallas_call(wgrad_kernel, out_shape=(jax.ShapeDtypeStruct(shape, F32),...  96.2 us
    pallas_call x17, Pallas kernels, update_units(): pl.pallas_call(functools.partial(update_kernel, n, len(chain), want_bf16)...  84.9 us
    pallas_call x1, Pallas kernels, backward(): pl.pallas_call(functools.partial(back_kernel, n_stages), name='backward',...  76.9 us
    pallas_call x1, Pallas kernels, clip_factor(): pl.pallas_call(functools.partial(norm_kernel, n_stages, n_rep), name='cli...  32.8 us
    ppermute x35, starting transfers between devices, exchange(): return lax.ppermute(x, 'data', swap)  31.6 us
    pallas_call x12, Pallas kernels, combine(): pl.pallas_call(functools.partial(combine_kernel, scale), name='combine',...  27.4 us
  transfers between devices with their start and end apart: 35, of which 15 were waited for; matrix products, arithmetic and copies ran while one was open for 0% of the time, Pallas kernels for 43%

profile of v2, /device:TPU:3, one launch (start us, length us, event | category | flops | bytes accessed | tf_op | source)
XLA Modules:
  0.0 762.9 jit_solution(2476006825930262588)
XLA Ops:
  0.6 76.9 %backward.1 = (bf16[4096,3072]{1,0:T(8,128)(2,1)}, bf16[4096,3072]{1,0:T(8,128)(2,1)}, bf16[4096,768]{1,0:T(8,128)(2,1)}) custom-call(bf16[1,4096,768]{2,1,0:T(8,128)(2,1)} %left_ref.9, bf16[4096,768]{1,0:T(8,128)(2,1)} %dy_ref.1, f32[1,768,3072]{2,1,0:T(8,128)} %w_ref.33, f32[1,3072,768]{2,1,0:T(8,128)} %w_ref.32), custom_call_target="tpu_custom_call" | custom-call | flops 57982058496 | bytes 75497472 | tf_op jit(solution)/shard_map/backward/pallas_call | solution.py:259
  83.9 9.2 %shard_map.182 = (f32[256,768]{1,0:T(8,128)}, f32[256,768]{1,0:T(8,128)}) custom-call(s32[1]{0:T(128)S(6)} %sub.3.owner_ref, bf16[4096,3072]{1,0:T(8,128)(2,1)} %get-tuple-element.144.left_ref, bf16[4096,768]{1,0:T(8,128)(2,1)} %get-tuple-element.145.right_ref, f32[1,1,3072,768]{3,2,1,0:T(8,128)} %grad_ref.17), custom_call_target="tpu_custom_call" | custom-call | flops 3221225472 | bytes 15728640 | tf_op jit(solution)/shard_map/pallas_call | solution.py:331
  93.1 8.9 %shard_map.183 = (f32[384,512]{1,0:T(8,128)}, f32[384,512]{1,0:T(8,128)}) custom-call(s32[1]{0:T(128)S(6)} %sub.3.owner_ref, bf16[1,4096,768]{2,1,0:T(8,128)(2,1)} %left_ref.9, bf16[4096,3072]{1,0:T(8,128)(2,1)} %get-tuple-element.141.right_ref, f32[1,1,768,3072]{3,2,1,0:T(8,128)} %grad_ref.16), custom_call_target="tpu_custom_call" | custom-call | flops 3221225472 | bytes 15728640 | tf_op jit(solution)/shard_map/pallas_call | solution.py:331
  101.9 9.2 %shard_map.184 = (f32[256,768]{1,0:T(8,128)}, f32[256,768]{1,0:T(8,128)}) custom-call(s32[1]{0:T(128)S(6)} %sub.3.owner_ref, bf16[4096,3072]{1,0:T(8,128)(2,1)} %get-tuple-element.144.left_ref, bf16[4096,768]{1,0:T(8,128)(2,1)} %get-tuple-element.145.right_ref, f32[1,1,3072,768]{3,2,1,0:T(8,128)} %grad_ref.17), custom_call_target="tpu_custom_call" | custom-call | flops 3221225472 | bytes 15728640 | tf_op jit(solution)/shard_map/pallas_call | solution.py:331
  115.9 8.9 %shard_map.185 = (f32[384,512]{1,0:T(8,128)}, f32[384,512]{1,0:T(8,128)}) custom-call(s32[1]{0:T(128)S(6)} %sub.3.owner_ref, bf16[1,4096,768]{2,1,0:T(8,128)(2,1)} %left_ref.9, bf16[4096,3072]{1,0:T(8,128)(2,1)} %get-tuple-element.141.right_ref, f32[1,1,768,3072]{3,2,1,0:T(8,128)} %grad_ref.16), custom_call_target="tpu_custom_call" | custom-call | flops 3221225472 | bytes 15728640 | tf_op jit(solution)/shard_map/pallas_call | solution.py:331
  124.8 9.3 %shard_map.186 = (f32[256,768]{1,0:T(8,128)}, f32[256,768]{1,0:T(8,128)}) custom-call(s32[1]{0:T(128)S(6)} %sub.3.owner_ref, bf16[4096,3072]{1,0:T(8,128)(2,1)} %get-tuple-element.144.left_ref, bf16[4096,768]{1,0:T(8,128)(2,1)} %get-tuple-element.145.right_ref, f32[1,1,3072,768]{3,2,1,0:T(8,128)} %grad_ref.17), custom_call_target="tpu_custom_call" | custom-call | flops 3221225472 | bytes 15728640 | tf_op jit(solution)/shard_map/pallas_call | solution.py:331
  142.5 19.0 %shard_map.180 = (f32[384,512]{1,0:T(8,128)}, f32[384,512]{1,0:T(8,128)}, f32[384,512]{1,0:T(8,128)}, f32[384,512]{1,0:T(8,128)}, f32[384,512]{1,0:T(8,128)}, /*index=5*/f32[384,512]{1,0:T(8,128)}) custom-call(s32[1]{0:T(128)} %bitcast.owner_ref, bf16[1,4096,768]{2,1,0:T(8,128)(2,1)} %left_ref.9, bf16[4096,3072]{1,0:T(8,128)(2,1)} %get-tuple-element.141.right_ref, ...), custom_call_target="tpu_custom_call" | custom-call | flops 9663676416 | bytes 15728640 | tf_op jit(solution)/shard_map/pallas_call | solution.py:331
  161.6 43.8 %collective-permute-done.7.theirs_ref = f32[384,512]{1,0:T(8,128)} collective-permute-done((f32[384,512]{1,0:T(8,128)}, f32[384,512]{1,0:T(8,128)}, u32[]{:S(2)}, u32[]{:S(2)}) %collective-permute-start.7) | collective-permute-done | bytes 786464 | tf_op jit(solution)/shard_map/ppermute | solution.py:658
  206.8 15.4 %collective-permute-done.9.theirs_ref = f32[256,768]{1,0:T(8,128)} collective-permute-done((f32[256,768]{1,0:T(8,128)}, f32[256,768]{1,0:T(8,128)}, u32[]{:S(2)}, u32[]{:S(2)}) %collective-permute-start.9) | collective-permute-done | bytes 786464 | tf_op jit(solution)/shard_map/ppermute | solution.py:658
  224.9 19.1 %shard_map.188 = (f32[256,768]{1,0:T(8,128)}, f32[256,768]{1,0:T(8,128)}, f32[256,768]{1,0:T(8,128)}, f32[256,768]{1,0:T(8,128)}, f32[256,768]{1,0:T(8,128)}, /*index=5*/f32[256,768]{1,0:T(8,128)}) custom-call(s32[1]{0:T(128)} %bitcast.owner_ref, bf16[4096,3072]{1,0:T(8,128)(2,1)} %get-tuple-element.144.left_ref, ...), custom_call_target="tpu_custom_call" | custom-call | flops 9663676416 | bytes 15728640 | tf_op jit(solution)/shard_map/pallas_call | solution.py:331
  262.9 43.5 %collective-permute-done.3.theirs_ref = f32[384,512]{1,0:T(8,128)} collective-permute-done((f32[384,512]{1,0:T(8,128)}, f32[384,512]{1,0:T(8,128)}, u32[]{:S(2)}, u32[]{:S(2)}) %collective-permute-start.3) | collective-permute-done | bytes 786464 | tf_op jit(solution)/shard_map/ppermute | solution.py:658
  317.3 32.8 %clip_factor.1.clip_ref = f32[8,128]{1,0:T(8,128)} custom-call(f32[8,128]{1,0:T(8,128)} %get-tuple-element.183.sq_ref, f32[1]{0:T(128)} %bitcast.22.max_ref), custom_call_target="tpu_custom_call" | custom-call | flops 40000000 | bytes 4096 | tf_op jit(solution)/shard_map/clip_factor/pallas_call | solution.py:485
  391.3 7.2 collective-permute-done.28.refs_17_
  416.6 7.2 collective-permute-done.31.refs_20_
  425.1 40.9 %collective-permute-done.32.refs_21_ = bf16[256,768]{1,0:T(8,128)(2,1)S(1)} collective-permute-done((bf16[256,768]{1,0:T(8,128)(2,1)}, bf16[256,768]{1,0:T(8,128)(2,1)S(1)}, u32[]{:S(2)}, u32[]{:S(2)}) %collective-permute-start.32) | collective-permute-done | bytes 393248 | tf_op jit(solution)/shard_map/ppermute | solution.py:658
  467.1 7.2 collective-permute-done.33.refs_22_
  475.5 7.2 collective-permute-done.34.refs_23_
  500.9 15.7 %collective-permute-done.14.rest_2_ = f32[256,768]{1,0:T(8,128)} collective-permute-done((f32[256,768]{1,0:T(8,128)S(1)}, f32[256,768]{1,0:T(8,128)}, u32[]{:S(2)}, u32[]{:S(2)}) %collective-permute-start.14) | collective-permute-done | bytes 786464 | tf_op jit(solution)/shard_map/ppermute | solution.py:658
  517.8 15.7 %collective-permute-done.15.rest_3_ = f32[256,768]{1,0:T(8,128)} collective-permute-done((f32[256,768]{1,0:T(8,128)S(1)}, f32[256,768]{1,0:T(8,128)}, u32[]{:S(2)}, u32[]{:S(2)}) %collective-permute-start.15) | collective-permute-done | bytes 786464 | tf_op jit(solution)/shard_map/ppermute | solution.py:658
  534.6 15.7 %collective-permute-done.16.rest_0_ = f32[384,512]{1,0:T(8,128)} collective-permute-done((f32[384,512]{1,0:T(8,128)}, f32[384,512]{1,0:T(8,128)}, u32[]{:S(2)}, u32[]{:S(2)}) %collective-permute-start.16) | collective-permute-done | bytes 786464 | tf_op jit(solution)/shard_map/ppermute | solution.py:658
  551.5 15.6 %collective-permute-done.17.rest_1_ = f32[384,512]{1,0:T(8,128)S(1)} collective-permute-done((f32[384,512]{1,0:T(8,128)S(1)}, f32[384,512]{1,0:T(8,128)S(1)}, u32[]{:S(2)}, u32[]{:S(2)}) %collective-permute-start.17) | collective-permute-done | bytes 786464 | tf_op jit(solution)/shard_map/ppermute | solution.py:658
  568.2 157.2 %forward.1.y_ref = bf16[8192,768]{1,0:T(8,128)(2,1)S(1)} custom-call(bf16[8192,768]{1,0:T(8,128)(2,1)} %bitcast.24, bf16[384,512]{1,0:T(8,128)(2,1)} %get-tuple-element.263.refs_0_, bf16[384,512]{1,0:T(8,128)(2,1)} %get-tuple-element.264.refs_1_, bf16[384,512]{1,0:T(8,128)(2,1)} %get-tuple-element.265.refs_2_, bf16[384,512]{1,0:T(8,128)(2,1)} %get-tuple-element.266.refs_3_, ...), custom_call_target="tpu_custom_call" | custom-call | flops 77309411328 | bytes 75497472 | tf_op jit(solution)/shard_map/forward/pallas_call | solution.py:605
  730.2 10.9 %shard_map.200 = (f32[1,3072,768]{2,1,0:T(8,128)}, f32[1,3072,768]{2,1,0:T(8,128)}, f32[1,3072,768]{2,1,0:T(8,128)}, f32[8,128]{1,0:T(8,128)}) custom-call(s32[1]{0:T(128)S(6)} %sub.3.owner_ref, f32[1]{0:T(128)} %bitcast.16.lr_ref, f32[8,128]{1,0:T(8,128)} %clip_factor.1.clip_ref, ...), custom_call_target="tpu_custom_call", output_to_operand_aliasing={{0}: (10, {}), {1}: (11, {}), {2}: (12, {})} | custom-call | flops 23592960 | bytes 22020096 | tf_op jit(solution)/shard_map/pallas_call | solution.py:440
  741.1 11.5 %shard_map.203 = (f32[1,768,3072]{2,1,0:T(8,128)}, f32[1,768,3072]{2,1,0:T(8,128)}, f32[1,768,3072]{2,1,0:T(8,128)}, f32[8,128]{1,0:T(8,128)}) custom-call(s32[1]{0:T(128)S(6)} %sub.3.owner_ref, f32[1]{0:T(128)} %bitcast.19.lr_ref, f32[8,128]{1,0:T(8,128)} %get-tuple-element.230.clip_ref, ...), custom_call_target="tpu_custom_call", output_to_operand_aliasing={{0}: (10, {}), {1}: (11, {}), {2}: (12, {})} | custom-call | flops 23592960 | bytes 22020096 | tf_op jit(solution)/shard_map/pallas_call | solution.py:440
  (129 shorter events, 152.8 us)
Async XLA Ops:
  112.6 94.0 %collective-permute-start.8 = (f32[384,512]{1,0:T(8,128)}, f32[384,512]{1,0:T(8,128)S(1)}, u32[]{:S(2)}, u32[]{:S(2)}) collective-permute-start(f32[384,512]{1,0:T(8,128)} %get-tuple-element.148), channel_id=1, source_target_pairs={{0,4},{4,0},{1,5},{5,1},{2,6},{6,2},{3,7},{7,3}} | collective-permute-start | bytes 2359304 | tf_op jit(solution)/shard_map/ppermute | solution.py:658
  113.8 109.6 %collective-permute-start.10 = (f32[256,768]{1,0:T(8,128)}, f32[256,768]{1,0:T(8,128)S(1)}, u32[]{:S(2)}, u32[]{:S(2)}) collective-permute-start(f32[256,768]{1,0:T(8,128)} %get-tuple-element.146), channel_id=1, source_target_pairs={{0,4},{4,0},{1,5},{5,1},{2,6},{6,2},{3,7},{7,3}} | collective-permute-start | bytes 2359304 | tf_op jit(solution)/shard_map/ppermute | solution.py:658
  114.0 109.6 %collective-permute-start.11 = (f32[384,512]{1,0:T(8,128)}, f32[384,512]{1,0:T(8,128)}, u32[]{:S(2)}, u32[]{:S(2)}) collective-permute-start(f32[384,512]{1,0:T(8,128)} %shard_map.181), channel_id=1, source_target_pairs={{0,4},{4,0},{1,5},{5,1},{2,6},{6,2},{3,7},{7,3}} | collective-permute-start | bytes 2359304 | tf_op jit(solution)/shard_map/ppermute | solution.py:658
  141.1 64.3 %collective-permute-start.7 = (f32[384,512]{1,0:T(8,128)}, f32[384,512]{1,0:T(8,128)}, u32[]{:S(2)}, u32[]{:S(2)}) collective-permute-start(f32[384,512]{1,0:T(8,128)} %get-tuple-element.166), channel_id=1, source_target_pairs={{0,4},{4,0},{1,5},{5,1},{2,6},{6,2},{3,7},{7,3}} | collective-permute-start | bytes 2359304 | tf_op jit(solution)/shard_map/ppermute | solution.py:658
  141.3 80.9 %collective-permute-start.9 = (f32[256,768]{1,0:T(8,128)}, f32[256,768]{1,0:T(8,128)}, u32[]{:S(2)}, u32[]{:S(2)}) collective-permute-start(f32[256,768]{1,0:T(8,128)} %get-tuple-element.169), channel_id=1, source_target_pairs={{0,4},{4,0},{1,5},{5,1},{2,6},{6,2},{3,7},{7,3}} | collective-permute-start | bytes 2359304 | tf_op jit(solution)/shard_map/ppermute | solution.py:658
  205.3 103.4 %collective-permute-start.2 = (f32[256,768]{1,0:T(8,128)}, f32[256,768]{1,0:T(8,128)S(1)}, u32[]{:S(2)}, u32[]{:S(2)}) collective-permute-start(f32[256,768]{1,0:T(8,128)} %get-tuple-element.154), channel_id=1, source_target_pairs={{0,4},{4,0},{1,5},{5,1},{2,6},{6,2},{3,7},{7,3}} | collective-permute-start | bytes 2359304 | tf_op jit(solution)/shard_map/ppermute | solution.py:658
  206.6 54.0 %collective-permute-start.4 = (f32[384,512]{1,0:T(8,128)}, f32[384,512]{1,0:T(8,128)}, u32[]{:S(2)}, u32[]{:S(2)}) collective-permute-start(f32[384,512]{1,0:T(8,128)} %get-tuple-element.152), channel_id=1, source_target_pairs={{0,4},{4,0},{1,5},{5,1},{2,6},{6,2},{3,7},{7,3}} | collective-permute-start | bytes 2359304 | tf_op jit(solution)/shard_map/ppermute | solution.py:658
  222.2 92.0 %collective-permute-start = (f32[384,512]{1,0:T(8,128)}, f32[384,512]{1,0:T(8,128)S(1)}, u32[]{:S(2)}, u32[]{:S(2)}) collective-permute-start(f32[384,512]{1,0:T(8,128)} %shard_map.187), channel_id=1, source_target_pairs={{0,4},{4,0},{1,5},{5,1},{2,6},{6,2},{3,7},{7,3}} | collective-permute-start | bytes 2359304 | tf_op jit(solution)/shard_map/ppermute | solution.py:658
  223.4 88.4 %collective-permute-start.1 = (f32[256,768]{1,0:T(8,128)}, f32[256,768]{1,0:T(8,128)}, u32[]{:S(2)}, u32[]{:S(2)}) collective-permute-start(f32[256,768]{1,0:T(8,128)} %get-tuple-element.157), channel_id=1, source_target_pairs={{0,4},{4,0},{1,5},{5,1},{2,6},{6,2},{3,7},{7,3}} | collective-permute-start | bytes 2359304 | tf_op jit(solution)/shard_map/ppermute | solution.py:658
  223.7 82.8 %collective-permute-start.3 = (f32[384,512]{1,0:T(8,128)}, f32[384,512]{1,0:T(8,128)}, u32[]{:S(2)}, u32[]{:S(2)}) collective-permute-start(f32[384,512]{1,0:T(8,128)} %get-tuple-element.160), channel_id=1, source_target_pairs={{0,4},{4,0},{1,5},{5,1},{2,6},{6,2},{3,7},{7,3}} | collective-permute-start | bytes 2359304 | tf_op jit(solution)/shard_map/ppermute | solution.py:658
  390.1 93.9 %collective-permute-start.12 = (f32[256,768]{1,0:T(8,128)}, f32[256,768]{1,0:T(8,128)}, u32[]{:S(2)}, u32[]{:S(2)}) collective-permute-start(f32[256,768]{1,0:T(8,128)} %get-tuple-element.203.rest_0_), channel_id=1, source_target_pairs={{0,4},{4,0},{1,5},{5,1},{2,6},{6,2},{3,7},{7,3}} | collective-permute-start | bytes 2359304 | tf_op jit(solution)/shard_map/ppermute | solution.py:658
  398.5 85.7 %collective-permute-start.20 = (f32[384,512]{1,0:T(8,128)S(1)}, f32[384,512]{1,0:T(8,128)}, u32[]{:S(2)}, u32[]{:S(2)}) collective-permute-start(f32[384,512]{1,0:T(8,128)S(1)} %copy-done.2), channel_id=1, source_target_pairs={{0,4},{4,0},{1,5},{5,1},{2,6},{6,2},{3,7},{7,3}} | collective-permute-start | bytes 2359304 | tf_op jit(solution)/shard_map/ppermute | solution.py:658
  411.4 54.5 %collective-permute-start.32 = (bf16[256,768]{1,0:T(8,128)(2,1)}, bf16[256,768]{1,0:T(8,128)(2,1)S(1)}, u32[]{:S(2)}, u32[]{:S(2)}) collective-permute-start(bf16[256,768]{1,0:T(8,128)(2,1)} %get-tuple-element.271.refs_9_), channel_id=1, source_target_pairs={{0,4},{4,0},{1,5},{5,1},{2,6},{6,2},{3,7},{7,3}} | collective-permute-start | bytes 1179656 | tf_op jit(solution)/shard_map/ppermute | solution.py:658
  415.5 58.9 %collective-permute-start.33 = (bf16[256,768]{1,0:T(8,128)(2,1)}, bf16[256,768]{1,0:T(8,128)(2,1)S(1)}, u32[]{:S(2)}, u32[]{:S(2)}) collective-permute-start(bf16[256,768]{1,0:T(8,128)(2,1)} %get-tuple-element.272.refs_10_), channel_id=1, source_target_pairs={{0,4},{4,0},{1,5},{5,1},{2,6},{6,2},{3,7},{7,3}} | collective-permute-start | bytes 1179656 | tf_op jit(solution)/shard_map/ppermute | solution.py:658
  423.9 58.9 %collective-permute-start.34 = (bf16[256,768]{1,0:T(8,128)(2,1)}, bf16[256,768]{1,0:T(8,128)(2,1)S(1)}, u32[]{:S(2)}, u32[]{:S(2)}) collective-permute-start(bf16[256,768]{1,0:T(8,128)(2,1)} %get-tuple-element.273.refs_11_), channel_id=1, source_target_pairs={{0,4},{4,0},{1,5},{5,1},{2,6},{6,2},{3,7},{7,3}} | collective-permute-start | bytes 1179656 | tf_op jit(solution)/shard_map/ppermute | solution.py:658
  474.3 42.2 %collective-permute-start.14 = (f32[256,768]{1,0:T(8,128)S(1)}, f32[256,768]{1,0:T(8,128)}, u32[]{:S(2)}, u32[]{:S(2)}) collective-permute-start(f32[256,768]{1,0:T(8,128)S(1)} %copy-done.4), channel_id=1, source_target_pairs={{0,4},{4,0},{1,5},{5,1},{2,6},{6,2},{3,7},{7,3}} | collective-permute-start | bytes 2359304 | tf_op jit(solution)/shard_map/ppermute | solution.py:658
  482.8 50.7 %collective-permute-start.15 = (f32[256,768]{1,0:T(8,128)S(1)}, f32[256,768]{1,0:T(8,128)}, u32[]{:S(2)}, u32[]{:S(2)}) collective-permute-start(f32[256,768]{1,0:T(8,128)S(1)} %copy-done.3), channel_id=1, source_target_pairs={{0,4},{4,0},{1,5},{5,1},{2,6},{6,2},{3,7},{7,3}} | collective-permute-start | bytes 2359304 | tf_op jit(solution)/shard_map/ppermute | solution.py:658
  484.0 66.3 %collective-permute-start.16 = (f32[384,512]{1,0:T(8,128)}, f32[384,512]{1,0:T(8,128)}, u32[]{:S(2)}, u32[]{:S(2)}) collective-permute-start(f32[384,512]{1,0:T(8,128)} %get-tuple-element.231.rest_0_), channel_id=1, source_target_pairs={{0,4},{4,0},{1,5},{5,1},{2,6},{6,2},{3,7},{7,3}} | collective-permute-start | bytes 2359304 | tf_op jit(solution)/shard_map/ppermute | solution.py:658
  484.2 82.8 %collective-permute-start.17 = (f32[384,512]{1,0:T(8,128)S(1)}, f32[384,512]{1,0:T(8,128)S(1)}, u32[]{:S(2)}, u32[]{:S(2)}) collective-permute-start(f32[384,512]{1,0:T(8,128)S(1)} %copy-done), channel_id=1, source_target_pairs={{0,4},{4,0},{1,5},{5,1},{2,6},{6,2},{3,7},{7,3}} | collective-permute-start | bytes 2359304 | tf_op jit(solution)/shard_map/ppermute | solution.py:658
  499.7 241.4 %collective-permute-start.18 = (f32[384,512]{1,0:T(8,128)}, f32[384,512]{1,0:T(8,128)}, u32[]{:S(2)}, u32[]{:S(2)}) collective-permute-start(f32[384,512]{1,0:T(8,128)} %get-tuple-element.233.rest_0_), channel_id=1, source_target_pairs={{0,4},{4,0},{1,5},{5,1},{2,6},{6,2},{3,7},{7,3}} | collective-permute-start | bytes 2359304 | tf_op jit(solution)/shard_map/ppermute | solution.py:658
  516.6 224.5 %collective-permute-start.19 = (f32[384,512]{1,0:T(8,128)}, f32[384,512]{1,0:T(8,128)}, u32[]{:S(2)}, u32[]{:S(2)}) collective-permute-start(f32[384,512]{1,0:T(8,128)} %get-tuple-element.234.rest_0_), channel_id=1, source_target_pairs={{0,4},{4,0},{1,5},{5,1},{2,6},{6,2},{3,7},{7,3}} | collective-permute-start | bytes 2359304 | tf_op jit(solution)/shard_map/ppermute | solution.py:658
  533.4 219.2 %collective-permute-start.21 = (f32[256,768]{1,0:T(8,128)}, f32[256,768]{1,0:T(8,128)}, u32[]{:S(2)}, u32[]{:S(2)}) collective-permute-start(f32[256,768]{1,0:T(8,128)} %get-tuple-element.247.rest_0_), channel_id=1, source_target_pairs={{0,4},{4,0},{1,5},{5,1},{2,6},{6,2},{3,7},{7,3}} | collective-permute-start | bytes 2359304 | tf_op jit(solution)/shard_map/ppermute | solution.py:658
  550.3 202.3 %collective-permute-start.22 = (f32[256,768]{1,0:T(8,128)}, f32[256,768]{1,0:T(8,128)}, u32[]{:S(2)}, u32[]{:S(2)}) collective-permute-start(f32[256,768]{1,0:T(8,128)} %get-tuple-element.248.rest_0_), channel_id=1, source_target_pairs={{0,4},{4,0},{1,5},{5,1},{2,6},{6,2},{3,7},{7,3}} | collective-permute-start | bytes 2359304 | tf_op jit(solution)/shard_map/ppermute | solution.py:658
  567.0 191.7 %collective-permute-start.23 = (f32[384,512]{1,0:T(8,128)}, f32[384,512]{1,0:T(8,128)}, u32[]{:S(2)}, u32[]{:S(2)}) collective-permute-start(f32[384,512]{1,0:T(8,128)} %get-tuple-element.253.rest_0_), channel_id=1, source_target_pairs={{0,4},{4,0},{1,5},{5,1},{2,6},{6,2},{3,7},{7,3}} | collective-permute-start | bytes 2359304 | tf_op jit(solution)/shard_map/ppermute | solution.py:658
  (31 other events, 807.1 us)
